TPU v7x, 32 devices: a whole 2x2x4 slice. The times are simulated.
32 devices in a mesh: rows: 8 (over z, y), grp: 4 (over x, core).
Axes of the slice: x: 2, y: 2, z: 4, core: 2. Of those that a mesh axis runs over, the one named last changes fastest.
Arguments:
- table: float32 [65536, 256], P(('rows', 'grp')), may hold values from -1.5 to 1.5
- hot_slot: int32 [512], P(('rows', 'grp')), may hold values from 0 to 2047, as said below
- cold_row: int32 [32, 32, 64], P(('rows', 'grp')), may hold values from 0 to 2047, as said below
- cold_bag: int32 [32, 32, 64], P(('rows', 'grp')), may hold values from 0 to 511
- hot_pick: int32 [8192, 8], P(('rows', 'grp')), may hold values from 0 to 511
- dense: float32 [8192, 256], P(('rows', 'grp')), may hold values from -6 to 6
- label: int32 [8192], P(('rows', 'grp')), may hold values 0 or 1
Outputs:
- pooled: float32 [8192, 256], P(('rows', 'grp'))
- new_table: float32 [65536, 256], P(('rows', 'grp'))
- hot_new: float32 [512, 256], replicated
Inputs may be any that keep to these rules, and one draw needn't show every extreme that they name: `hot_slot`: distinct within each device's block of 16 entries; hot row h lies in the shard of device h // 16. `cold_row`: a cold slot never names a hot row of its owner. `cold_bag`: a value of 256 or more marks an empty slot.
All inputs are finite; a program needn't handle non-finite values. No bound on the sum of `label` on one device may be relied on, other than what follows from the above.
Results may differ from a plain program's by a relative error of at most 0.0029.
Values may be sent and summed in bfloat16 or wider, within the bound.
No kernel may reach another device: no remote copies, remote signals or barrier semaphores. Data moves between devices by JAX's collectives and lax.ppermute only.
A program may use at most 64 MiB of HBM per device.

v0:
```python
import jax
import jax.numpy as jnp
from jax import lax
from jax.sharding import PartitionSpec as P


def body(table, hot_slot, cold_row, cold_bag, hot_pick, dense, label):
    n_rows = lax.axis_size("rows")
    n_grp = lax.axis_size("grp")
    width = table.shape[1]
    samples = dense.shape[0]
    own_hot = hot_slot.shape[0]
    slots = cold_row.shape[1] * cold_row.shape[2]
    per_peer = cold_row.shape[2]
    rounded = table.astype(jnp.bfloat16)
    hot_full = lax.all_gather(table[hot_slot], ("rows", "grp"), axis=0, tiled=True)
    hot_copy = hot_full.astype(jnp.bfloat16)
    requests = cold_row[0].reshape(n_rows, n_grp, per_peer)
    arrived = lax.all_to_all(
        lax.all_to_all(requests, "rows", split_axis=0, concat_axis=0, tiled=True),
        "grp",
        split_axis=1,
        concat_axis=1,
        tiled=True,
    )
    looked = rounded[arrived.reshape(-1)].reshape(n_rows, n_grp, per_peer, width)
    returned = lax.all_to_all(
        lax.all_to_all(looked, "rows", split_axis=0, concat_axis=0, tiled=True),
        "grp",
        split_axis=1,
        concat_axis=1,
        tiled=True,
    )
    flat_rows = returned.reshape(slots, width)
    bags = cold_bag[0].reshape(slots)
    selector = jnp.arange(samples, dtype=jnp.int32)[:, None] == bags[None, :]
    cold_pooled = jnp.dot(
        selector.astype(jnp.bfloat16), flat_rows, preferred_element_type=jnp.float32
    )
    hot_pooled = jnp.sum(hot_copy[hot_pick].astype(jnp.float32), axis=1)
    pooled = cold_pooled + hot_pooled
    score = jnp.sum(pooled * dense, axis=1) / width**0.5
    err = jax.nn.sigmoid(score) - label.astype(jnp.float32)
    grad = err[:, None] * dense
    slot_grad = lax.dot_general(
        selector.astype(jnp.float32),
        grad,
        (((0,), (0,)), ((), ())),
        precision=lax.Precision.HIGHEST,
        preferred_element_type=jnp.float32,
    )
    delivered = lax.all_to_all(
        lax.all_to_all(
            slot_grad.reshape(n_rows, n_grp, per_peer, width),
            "rows",
            split_axis=0,
            concat_axis=0,
            tiled=True,
        ),
        "grp",
        split_axis=1,
        concat_axis=1,
        tiled=True,
    )
    table_grad = jax.ops.segment_sum(
        delivered.reshape(slots, width), arrived.reshape(slots), num_segments=table.shape[0]
    )
    hot_total = hot_copy.shape[0]
    spread = jnp.repeat(grad, hot_pick.shape[1], axis=0)
    hot_local = jax.ops.segment_sum(spread, hot_pick.reshape(-1), num_segments=hot_total)
    quarter = lax.psum_scatter(hot_local, "grp", scatter_dimension=0, tiled=True)
    crossed = lax.psum(quarter, "rows")
    summed = lax.all_gather(crossed, "grp", axis=0, tiled=True)
    start = lax.axis_index(("rows", "grp")) * own_hot
    own_grad = lax.dynamic_slice_in_dim(summed, start, own_hot, 0)
    table_grad = table_grad.at[hot_slot].add(own_grad)
    new_table = table - 0.1 * table_grad
    hot_new = hot_full - 0.1 * summed
    return (pooled, new_table, hot_new)


def solution(mesh):
    placed = (
        P(("rows", "grp"), None),
        P(("rows", "grp")),
        P(("rows", "grp"), None, None),
        P(("rows", "grp"), None, None),
        P(("rows", "grp"), None),
        P(("rows", "grp"), None),
        P(("rows", "grp")),
    )
    return jax.shard_map(
        body,
        mesh=mesh,
        in_specs=placed,
        out_specs=(P(("rows", "grp"), None), P(("rows", "grp"), None), P()),
        check_vma=False,
    )
```

profile of v0, /device:TPU:0, one launch (start us, length us, event | category | flops | bytes accessed | tf_op | source)
XLA Modules:
  0.0 316.5 jit_solution(10149955036070640280)
XLA Ops:
  8.0 13.6 %all_to_all.30 = s32[8,1,256]{2,1,0:T(1,128)S(1)} all-to-all(s32[8,1,256]{2,1,0:T(1,128)S(1)} %reshape.122), channel_id=1, replica_groups=mesh['rows'=8,'grp'=4] {'rows'}, dimensions={0} | all-to-all | bytes 16384 | tf_op jit(solution)/shard_map/all_to_all | solution.py:20
  23.5 3.2 %all-to-all-start.1 = ((s32[4,1,512]{2,1,0:T(1,128)}), s32[4,1,512]{2,1,0:T(1,128)S(1)}, u32[]{:S(2)}, u32[]{:S(2)}) async-start(s32[4,1,512]{2,1,0:T(1,128)} %reshape.124), calls=%async_computation.1 | async-start | bytes 16384 | tf_op jit(solution)/shard_map/all_to_all | solution.py:19
  26.8 1.7 convert_element_type.14
  28.5 2.1 all-to-all-done.1
  31.5 9.1 %gather_fusion = bf16[2048,256]{1,0:T(8,128)(2,1)} fusion(bf16[2048,256]{1,0:T(8,128)(2,1)S(1)} %convert_element_type.14, s32[2048]{0:T(1024)S(1)} %broadcast_clamp_fusion.1), kind=kCustom, calls=%fused_computation | custom fusion | bytes 2105344 | tf_op jit(solution)/shard_map/gather | solution.py:26
  40.5 4.4 %all-to-all-start.2 = ((bf16[8,4,64,256]{3,2,1,0:T(8,128)(2,1)}), bf16[8,4,64,256]{3,2,1,0:T(8,128)(2,1)}, u32[]{:S(2)}, u32[]{:S(2)}) async-start(bf16[8,4,64,256]{3,2,1,0:T(8,128)(2,1)} %bitcast.19), calls=%async_computation.2 | async-start | bytes 2097152 | tf_op jit(solution)/shard_map/all_to_all | solution.py:28
  46.4 24.6 %all-to-all-done.2 = bf16[8,4,64,256]{3,2,1,0:T(8,128)(2,1)} async-done(((bf16[8,4,64,256]{3,2,1,0:T(8,128)(2,1)}), bf16[8,4,64,256]{3,2,1,0:T(8,128)(2,1)}, u32[]{:S(2)}, u32[]{:S(2)}) %all-to-all-start.2) | async-done | bytes 1048608 | tf_op jit(solution)/shard_map/all_to_all | solution.py:28
  70.9 2.3 copy.37
  73.2 4.4 %all-to-all-start.3 = ((bf16[8,4,64,256]{3,2,0,1:T(8,128)(2,1)}), bf16[8,4,64,256]{3,2,0,1:T(8,128)(2,1)}, u32[]{:S(2)}, u32[]{:S(2)}) async-start(bf16[8,4,64,256]{3,2,0,1:T(8,128)(2,1)} %copy.37), calls=%async_computation.3 | async-start | bytes 2097152 | tf_op jit(solution)/shard_map/all_to_all | solution.py:27
  77.6 46.8 %all-gather = f32[512,256]{1,0:T(8,128)S(1)} all-gather(f32[16,256]{1,0:T(8,128)S(1)} %gather_fusion.1), channel_id=2, replica_groups=mesh['rows'=8,'grp'=4] {'rows','grp'}, dimensions={0}, use_global_device_ids=true | all-gather | bytes 540672 | tf_op jit(solution)/shard_map/all_gather | solution.py:16
  124.8 9.1 %gather_fusion.2 = bf16[2048,256]{1,0:T(8,128)(2,1)} fusion(bf16[512,256]{1,0:T(8,128)(2,1)S(1)} %convert_element_type.15, s32[2048]{0:T(1024)S(1)} %broadcast_clamp_fusion), kind=kCustom, calls=%fused_computation.2 | custom fusion | bytes 2105344 | tf_op jit(solution)/shard_map/gather | solution.py:40
  133.8 1.9 convert_reduce_fusion
  139.8 3.2 fusion.2
  142.9 4.3 %all-to-all-start.4 = ((f32[8,4,64,256]{3,2,1,0:T(8,128)}), f32[8,4,64,256]{3,2,1,0:T(8,128)}, u32[]{:S(2)}, u32[]{:S(2)}) async-start(f32[8,4,64,256]{3,2,1,0:T(8,128)} %bitcast.18), calls=%async_computation.4 | async-start | bytes 4194304 | tf_op jit(solution)/shard_map/all_to_all | solution.py:53
  147.6 12.4 %scatter_custom_fusion.1 = f32[512,256]{1,0:T(8,128)} fusion(s32[2048]{0:T(1024)S(1)} %reshape.94, f32[256,256]{1,0:T(8,128)S(1)} %broadcast_multiply_fusion, f32[]{:T(128)} %constant.15.clone.1), kind=kCustom, calls=%fused_computation.7 | custom fusion | flops 524288 | bytes 786436 | tf_op jit(solution)/shard_map/scatter-add | solution.py:70
  160.0 36.3 %all-to-all-done.4 = f32[8,4,64,256]{3,2,1,0:T(8,128)} async-done(((f32[8,4,64,256]{3,2,1,0:T(8,128)}), f32[8,4,64,256]{3,2,1,0:T(8,128)}, u32[]{:S(2)}, u32[]{:S(2)}) %all-to-all-start.4) | async-done | bytes 2097184 | tf_op jit(solution)/shard_map/all_to_all | solution.py:53
  196.3 3.1 copy.43
  199.4 4.4 %all-to-all-start.5 = ((f32[8,4,64,256]{3,2,0,1:T(8,128)}), f32[8,4,64,256]{3,2,0,1:T(8,128)}, u32[]{:S(2)}, u32[]{:S(2)}) async-start(f32[8,4,64,256]{3,2,0,1:T(8,128)} %copy.43), calls=%async_computation.5 | async-start | bytes 4194304 | tf_op jit(solution)/shard_map/all_to_all | solution.py:52
  205.6 72.4 %all-reduce.2.cloned.1.call-done = f32[128,256]{1,0:T(8,128)} async-done(((f32[128,256]{1,0:T(8,128)}), f32[128,256]{1,0:T(8,128)}) %all-reduce.2.cloned.1.call-update) | async-done | bytes 131088 | tf_op jit(solution)/shard_map/psum | solution.py:72
  278.0 7.5 %all_gather.7 = f32[512,256]{1,0:T(8,128)S(1)} all-gather(f32[128,256]{1,0:T(8,128)} %all-reduce.2.cloned.1.call-done), channel_id=1, replica_groups=mesh['rows'=8,'grp'=4] {'grp'}, dimensions={0}, use_global_device_ids=true | all-gather | bytes 655360 | tf_op jit(solution)/shard_map/all_gather | solution.py:73
  286.4 3.1 copy.44
  289.5 13.4 %scatter_custom_fusion = f32[2048,256]{1,0:T(8,128)} fusion(s32[2048]{0:T(1024)S(1)} %reshape.86, f32[2048,256]{1,0:T(8,128)} %bitcast.20, f32[]{:T(128)} %constant.15.clone.1), kind=kCustom, calls=%fused_computation.15 | custom fusion | flops 524288 | bytes 2097664 | tf_op jit(solution)/shard_map/scatter-add | solution.py:65
  302.9 3.6 %scatter_custom_fusion.2 = f32[2048,256]{1,0:T(8,128)} fusion(f32[2048,256]{1,0:T(8,128)} %scatter_custom_fusion, s32[16]{0:T(128)S(1)} %compare_select_fusion.2, f32[512,256]{1,0:T(8,128)S(1)} %all_gather.7, s32[]{:T(128)S(6)} %select_n.23, s32[]{:T(128)} %constant.12.clone.1), kind=kCustom, calls=%fused_computation.25 | custom fusion | flops 4096 | bytes 2114052 | tf_op jit(solution)/shard_map/scatter-add | solution.py:76
  306.5 3.2 %multiply_subtract_fusion = f32[2048,256]{1,0:T(8,128)} fusion(f32[2048,256]{1,0:T(8,128)S(1)} %copy-done, f32[2048,256]{1,0:T(8,128)} %scatter_custom_fusion.2), kind=kLoop, calls=%fused_computation.9 | loop fusion | flops 1048576 | bytes 6291456 | tf_op jit(solution)/shard_map/sub | solution.py:77
  (53 shorter events, 12.1 us)
Async XLA Ops:
  23.5 7.0 %all-to-all-start.1 = ((s32[4,1,512]{2,1,0:T(1,128)}), s32[4,1,512]{2,1,0:T(1,128)S(1)}, u32[]{:S(2)}, u32[]{:S(2)}) async-start(s32[4,1,512]{2,1,0:T(1,128)} %reshape.124), calls=%async_computation.1 | async-start | bytes 16384 | tf_op jit(solution)/shard_map/all_to_all | solution.py:19
  31.5 13.5 %copy-start.1 = (f32[256,256]{1,0:T(8,128)S(1)}, f32[256,256]{1,0:T(8,128)}, u32[]{:S(2)}) copy-start(f32[256,256]{1,0:T(8,128)} %param.12) | copy-start | bytes 786436
  40.5 5.2 %copy-start.6 = (s32[16]{0:T(128)S(1)}, s32[16]{0:T(128)}, u32[]{:S(2)}) copy-start(s32[16]{0:T(128)} %param.8) | copy-start | bytes 196
  40.5 5.2 %copy-start = (f32[2048,256]{1,0:T(8,128)S(1)}, f32[2048,256]{1,0:T(8,128)}, u32[]{:S(2)}) copy-start(f32[2048,256]{1,0:T(8,128)} %param.7) | copy-start | bytes 6291460
  40.5 30.4 %all-to-all-start.2 = ((bf16[8,4,64,256]{3,2,1,0:T(8,128)(2,1)}), bf16[8,4,64,256]{3,2,1,0:T(8,128)(2,1)}, u32[]{:S(2)}, u32[]{:S(2)}) async-start(bf16[8,4,64,256]{3,2,1,0:T(8,128)(2,1)} %bitcast.19), calls=%async_computation.2 | async-start | bytes 2097152 | tf_op jit(solution)/shard_map/all_to_all | solution.py:28
  73.2 51.2 %copy-start.3 = (s32[256,8]{0,1:T(8,128)S(1)}, s32[256,8]{0,1:T(8,128)}, u32[]{:S(2)}) copy-start(s32[256,8]{0,1:T(8,128)} %param.11) | copy-start | bytes 24580
  73.2 63.4 %all-to-all-start.3 = ((bf16[8,4,64,256]{3,2,0,1:T(8,128)(2,1)}), bf16[8,4,64,256]{3,2,0,1:T(8,128)(2,1)}, u32[]{:S(2)}, u32[]{:S(2)}) async-start(bf16[8,4,64,256]{3,2,0,1:T(8,128)(2,1)} %copy.37), calls=%async_computation.3 | async-start | bytes 2097152 | tf_op jit(solution)/shard_map/all_to_all | solution.py:27
  124.7 11.8 %copy-start.4 = (s32[1,32,64]{2,1,0:T(8,128)S(1)}, s32[1,32,64]{2,1,0:T(8,128)}, u32[]{:S(2)}) copy-start(s32[1,32,64]{2,1,0:T(8,128)} %param.10) | copy-start | bytes 24580
  136.6 1.4 copy-start.2
  136.7 3.0 copy-start.5
  142.9 53.4 %all-to-all-start.4 = ((f32[8,4,64,256]{3,2,1,0:T(8,128)}), f32[8,4,64,256]{3,2,1,0:T(8,128)}, u32[]{:S(2)}, u32[]{:S(2)}) async-start(f32[8,4,64,256]{3,2,1,0:T(8,128)} %bitcast.18), calls=%async_computation.4 | async-start | bytes 4194304 | tf_op jit(solution)/shard_map/all_to_all | solution.py:53
  147.3 56.7 %reduce-scatter.2.cloned.1.call-start = ((), (), s32[]{:S(2)}) async-start(), calls=%async_computation.7 | async-start | bytes 655360 | tf_op jit(solution)/shard_map/reduce_scatter | solution.py:71
  199.4 86.9 %all-to-all-start.5 = ((f32[8,4,64,256]{3,2,0,1:T(8,128)}), f32[8,4,64,256]{3,2,0,1:T(8,128)}, u32[]{:S(2)}, u32[]{:S(2)}) async-start(f32[8,4,64,256]{3,2,0,1:T(8,128)} %copy.43), calls=%async_computation.5 | async-start | bytes 4194304 | tf_op jit(solution)/shard_map/all_to_all | solution.py:52
  203.9 74.1 %all-reduce.2.cloned.1.call-start = ((), (), s32[]{:S(2)}) async-start(), calls=%async_computation.8 | async-start | bytes 262144 | tf_op jit(solution)/shard_map/psum | solution.py:72
Sparse Core Ops, SparseCore 0:
  160.1 21.9 reduce-scatter.1
  208.1 69.8 all-reduce.1
where the time goes:
time: 317 us; the launch traced here: 316 us
  waiting for transfers between devices  136 us (43%)
  blocking collectives  67.9 us (21%)
  other arithmetic  38.5 us (12%)
  local copies, waits for them, and re-layouts  34 us (11%)
  starting transfers between devices  20.9 us (7%)
  between operations  14.3 us (5%)
  matrix products  4.82 us (2%)
    psum x1, waiting for transfers between devices, body(): crossed = lax.psum(quarter, 'rows')  72.4 us
    all_gather x1, blocking collectives, body(): lax.all_gather(table[hot_slot], ('rows', 'grp'), axis=0, tiled=True)  46.8 us
    all_to_all x1, waiting for transfers between devices, body(): lax.all_to_all(slot_grad.reshape(n_rows, n_grp, per_peer, width), 'rows',...  36.3 us
    all_to_all x1, waiting for transfers between devices, body(): lax.all_to_all(looked, 'rows', split_axis=0, concat_axis=0, tiled=True)  24.6 us
    all_to_all x1, blocking collectives, body(): lax.all_to_all(requests, 'rows', split_axis=0, concat_axis=0, tiled=True)  13.6 us
    scatter-add x1, other arithmetic, body(): jax.ops.segment_sum(delivered.reshape(slots, width), arrived.reshape(slot...  13.4 us
    scatter-add x1, other arithmetic, body(): jax.ops.segment_sum(spread, hot_pick.reshape(-1), num_segments=hot_total)  12.4 us
    gather x1, local copies, waits for them, and re-layouts, body(): rounded[arrived.reshape(-1)].reshape(n_rows, n_grp, per_peer, width)  9.06 us
  transfers between devices with their start and end apart: 7, of which 4 were waited for; matrix products, arithmetic and copies ran while one was open for 10% of the time, Pallas kernels for 0%

commit v1 on v0

v1 whole, which is shorter than its diff:
```python
import jax
import jax.numpy as jnp
from jax import lax
from jax.sharding import PartitionSpec as P

AXES = ("rows", "grp")


def exchange(x):
    return lax.all_to_all(x, AXES, split_axis=0, concat_axis=0, tiled=True)


def body(table, hot_slot, cold_row, cold_bag, hot_pick, dense, label):
    width = table.shape[1]
    samples = dense.shape[0]
    own_hot = hot_slot.shape[0]
    peers, per_peer = cold_row.shape[1], cold_row.shape[2]
    slots = peers * per_peer
    bf16 = jnp.bfloat16
    arrived = exchange(cold_row[0]).reshape(slots)
    rounded = table.astype(bf16)
    owned = jnp.arange(table.shape[0], dtype=jnp.int32)
    looked = rounded[arrived].reshape(peers, per_peer, width)
    hot_rows = table[hot_slot]
    shared = jnp.broadcast_to(hot_rows.astype(bf16)[None], (peers, own_hot, width))
    returned = exchange(jnp.concatenate([looked, shared], axis=1))
    cold_rows = returned[:, :per_peer].reshape(slots, width)
    hot_copy = returned[:, per_peer:].reshape(peers * own_hot, width)
    bags = cold_bag[0].reshape(slots)
    selector = (jnp.arange(samples, dtype=jnp.int32)[:, None] == bags[None, :]).astype(bf16)
    hot_total = peers * own_hot
    picks = jnp.sum(
        (hot_pick[:, :, None] == jnp.arange(hot_total, dtype=jnp.int32)).astype(jnp.float32), axis=1
    ).astype(bf16)
    pooled = jnp.dot(selector, cold_rows, preferred_element_type=jnp.float32) + jnp.dot(
        picks, hot_copy, preferred_element_type=jnp.float32
    )
    score = jnp.sum(pooled * dense, axis=1) / width**0.5
    err = jax.nn.sigmoid(score) - label.astype(jnp.float32)
    grad = (err[:, None] * dense).astype(bf16)
    over_samples = (((0,), (0,)), ((), ()))
    slot_grad = lax.dot_general(selector, grad, over_samples, preferred_element_type=jnp.float32)
    hot_part = lax.dot_general(picks, grad, over_samples, preferred_element_type=jnp.float32)
    sent = jnp.concatenate(
        [
            slot_grad.astype(bf16).reshape(peers, per_peer, width),
            hot_part.astype(bf16).reshape(peers, own_hot, width),
        ],
        axis=1,
    )
    delivered = exchange(sent)
    own_grad = jnp.sum(delivered[:, per_peer:].astype(jnp.float32), axis=0)
    placed = (owned[:, None] == arrived[None, :]).astype(bf16)
    table_grad = jnp.dot(
        placed, delivered[:, :per_peer].reshape(slots, width), preferred_element_type=jnp.float32
    )
    own_new = hot_rows - 0.1 * own_grad
    new_table = (table - 0.1 * table_grad).at[hot_slot].set(own_new)
    hot_new = exchange(jnp.broadcast_to(own_new[None], (peers, own_hot, width)))
    return (pooled, new_table, hot_new.reshape(hot_total, width))


def solution(mesh):
    placed = (
        P(AXES, None),
        P(AXES),
        P(AXES, None, None),
        P(AXES, None, None),
        P(AXES, None),
        P(AXES, None),
        P(AXES),
    )
    return jax.shard_map(
        body,
        mesh=mesh,
        in_specs=placed,
        out_specs=(P(AXES, None), P(AXES, None), P()),
        check_vma=False,
    )
```

time: 317 us -> 122 us (0.38)
  waiting for transfers between devices: 136 us -> 37.9 us
  other arithmetic: 38.5 us -> 6.06 us
  blocking collectives: 67.9 us -> 36.6 us
  local copies, waits for them, and re-layouts: 34 us -> 19 us
  between operations: 14.3 us -> 0.86 us
  starting transfers between devices: 20.9 us -> 14 us
    psum x1 -> x0, waiting for transfers between devices: 72.4 us -> none  [body(): crossed = lax.psum(quarter, 'rows')]
    all_gather x2 -> x0, blocking collectives: 54.3 us -> none  [the longest x1 46.8 us: body(): lax.all_gather(table[hot_slot], ('rows', 'grp'), axis=0, tiled=True)]
    scatter-add x3 -> x0, other arithmetic: 29.4 us -> none  [the longest x1 13.4 us: body(): jax.ops.segment_sum(delivered.reshape(slots, width), arrived.reshape(slot...]
    all_to_all x5 -> x3, waiting for transfers between devices: 63 us -> 37.9 us  [exchange(): return lax.all_to_all(x, AXES, split_axis=0, concat_axis=0, tiled=True)]
    all_to_all x1, blocking collectives: 13.6 us -> 36.6 us  [exchange(): return lax.all_to_all(x, AXES, split_axis=0, concat_axis=0, tiled=True)]
    all_to_all x7 -> x1, local copies, waits for them, and re-layouts: 10.4 us -> 0.51 us  [exchange(): return lax.all_to_all(x, AXES, split_axis=0, concat_axis=0, tiled=True)]
    gather x3 -> x2, local copies, waits for them, and re-layouts: 18.7 us -> 9.67 us  [the longest x1 7.5 us: body(): looked = rounded[arrived].reshape(peers, per_peer, width)]
    all_to_all x5 -> x3, starting transfers between devices: 20.8 us -> 14 us  [exchange(): return lax.all_to_all(x, AXES, split_axis=0, concat_axis=0, tiled=True)]
  transfers between devices with their start and end apart: 7 -> 3, of which waited for: 4 -> 3; matrix products, arithmetic and copies ran while one was open for 10% -> 14% of each run, Pallas kernels for 0% -> 0%
where the time goes in v1:
time: 122 us
  waiting for transfers between devices  37.9 us (31%)
  blocking collectives  36.6 us (30%)
  local copies, waits for them, and re-layouts  19 us (16%)
  starting transfers between devices  14 us (11%)
  matrix products  7.39 us (6%)
  other arithmetic  6.06 us (5%)
    all_to_all x3, waiting for transfers between devices, exchange(): return lax.all_to_all(x, AXES, split_axis=0, concat_axis=0, tiled=True)  37.9 us
    all_to_all x1, blocking collectives, exchange(): return lax.all_to_all(x, AXES, split_axis=0, concat_axis=0, tiled=True)  36.6 us
    all_to_all x3, starting transfers between devices, exchange(): return lax.all_to_all(x, AXES, split_axis=0, concat_axis=0, tiled=True)  14 us
    gather x1, local copies, waits for them, and re-layouts, body(): looked = rounded[arrived].reshape(peers, per_peer, width)  7.5 us
    dot_general x1, matrix products, body(): jnp.dot(placed, delivered[:, :per_peer].reshape(slots, width), preferred_...  4.58 us
    unnamed x14, local copies, waits for them, and re-layouts  3.94 us
    scatter x1, local copies, waits for them, and re-layouts, body(): new_table = (table - 0.1 * table_grad).at[hot_slot].set(own_new)  3.51 us
  transfers between devices with their start and end apart: 3, of which 3 were waited for; matrix products, arithmetic and copies ran while one was open for 14% of the time, Pallas kernels for 0%

profile of v1, /device:TPU:0, one launch (start us, length us, event | category | flops | bytes accessed | tf_op | source)
XLA Modules:
  0.0 121.8 jit_solution(13687075481173957010)
XLA Ops:
  0.6 7.3 %all-to-all-start = ((s32[32,1,64]{2,1,0:T(1,128)}), s32[32,1,64]{2,1,0:T(1,128)S(1)}, u32[]{:S(2)}, u32[]{:S(2)}) async-start(s32[32,1,64]{2,1,0:T(1,128)} %bitcast.23), calls=%async_computation | async-start | bytes 32768 | tf_op jit(solution)/shard_map/all_to_all | solution.py:10
  8.0 0.7 compare_select_fusion.1
  8.6 1.7 %convert_element_type.33 = bf16[2048,256]{1,0:T(8,128)(2,1)S(1)} convert(f32[2048,256]{1,0:T(8,128)} %param.7) | non-fusion elementwise | flops 524288 | bytes 3145728 | tf_op jit(solution)/shard_map/convert_element_type | solution.py:21
  10.3 2.2 %gather_fusion.1 = f32[16,256]{1,0:T(8,128)S(1)} fusion(f32[2048,256]{1,0:T(8,128)} %param.7, s32[1024]{0:T(1024)S(1)} %pad_clamp_fusion), kind=kCustom, calls=%fused_computation.1 | custom fusion | bytes 32832 | tf_op jit(solution)/shard_map/gather | solution.py:24
  12.5 2.6 %all-to-all-done = s32[32,1,64]{2,1,0:T(1,128)S(1)} async-done(((s32[32,1,64]{2,1,0:T(1,128)}), s32[32,1,64]{2,1,0:T(1,128)S(1)}, u32[]{:S(2)}, u32[]{:S(2)}) %all-to-all-start) | async-done | bytes 8224 | tf_op jit(solution)/shard_map/all_to_all | solution.py:10
  15.1 0.5 broadcast.49
  15.6 0.7 reduce.5
  16.4 7.5 %gather_fusion = bf16[2048,256]{1,0:T(8,128)(2,1)S(1)} fusion(bf16[2048,256]{1,0:T(8,128)(2,1)S(1)} %convert_element_type.33, s32[2048]{0:T(1024)S(1)} %broadcast_clamp_fusion), kind=kCustom, calls=%fused_computation | custom fusion | bytes 2105344 | tf_op jit(solution)/shard_map/gather | solution.py:23
  24.0 1.1 pad_maximum_fusion
  25.1 3.3 %all-to-all-start.1 = ((bf16[32,80,256]{2,1,0:T(8,128)(2,1)}), bf16[32,80,256]{2,1,0:T(8,128)(2,1)S(1)}, u32[]{:S(2)}, u32[]{:S(2)}) async-start(bf16[32,80,256]{2,1,0:T(8,128)(2,1)} %pad_maximum_fusion), calls=%async_computation.1 | async-start | bytes 2621440 | tf_op jit(solution)/shard_map/all_to_all | solution.py:10
  28.8 1.7 %convert_reduce_fusion = bf16[256,512]{1,0:T(8,128)(2,1)S(1)} fusion(s32[256,8]{1,0:T(8,128)S(1)} %copy.16), kind=kLoop, calls=%fused_computation.6 | loop fusion | flops 3014656 | bytes 270336 | tf_op jit(solution)/shard_map/reduce_sum | solution.py:32
  30.5 29.9 %all-to-all-done.1 = bf16[32,80,256]{2,1,0:T(8,128)(2,1)S(1)} async-done(((bf16[32,80,256]{2,1,0:T(8,128)(2,1)}), bf16[32,80,256]{2,1,0:T(8,128)(2,1)S(1)}, u32[]{:S(2)}, u32[]{:S(2)}) %all-to-all-start.1) | async-done | bytes 1310752 | tf_op jit(solution)/shard_map/all_to_all | solution.py:10
  60.5 0.7 fusion.4
  61.2 1.0 multiply_reduce_fusion
  62.2 0.8 convolution_convert_fusion
  63.0 0.3 convolution_convert_fusion.1
  63.5 36.6 %all_to_all.24 = bf16[32,80,256]{2,1,0:T(8,128)(2,1)S(1)} all-to-all(bf16[32,80,256]{2,1,0:T(8,128)(2,1)S(1)} %pad_maximum_fusion.1), channel_id=1, replica_groups=mesh['rows'=8,'grp'=4] {'rows','grp'}, dimensions={0} | all-to-all | bytes 2621440 | tf_op jit(solution)/shard_map/all_to_all | solution.py:10
  100.2 0.9 broadcast_in_dim.8
  101.0 3.3 %all-to-all-start.3 = ((f32[32,16,256]{2,1,0:T(8,128)}), f32[32,16,256]{2,1,0:T(8,128)}, u32[]{:S(2)}, u32[]{:S(2)}) async-start(f32[32,16,256]{2,1,0:T(8,128)} %broadcast_in_dim.8), calls=%async_computation.3 | async-start | bytes 1048576 | tf_op jit(solution)/shard_map/all_to_all | solution.py:10
  104.4 1.8 %copy.18 = f32[256,256]{1,0:T(8,128)} copy(f32[256,256]{0,1:T(8,128)} %get-tuple-element.13) | data formatting | bytes 524288
  106.4 4.6 %fusion.3 = f32[2048,256]{1,0:T(8,128)} fusion(f32[2048,256]{1,0:T(8,128)S(1)} %copy-done, bf16[2048,256]{1,0:T(8,128)(2,1)S(1)} %bitcast.18, s32[2048]{0:T(1024)S(1)} %eq.51), kind=kOutput, calls=%fused_computation.9 | convolution fusion | flops 2152726528 | bytes 5251072 | tf_op jit(solution)/shard_map/dot_general | solution.py:54
  110.9 3.5 %scatter_fusion = f32[2048,256]{1,0:T(8,128)} fusion(f32[2048,256]{1,0:T(8,128)} %fusion.3, s32[16]{0:T(128)S(1)} %compare_select_fusion.1, f32[16,256]{1,0:T(8,128)S(1)} %multiply_subtract_fusion), kind=kCustom, calls=%fused_computation.2 | custom fusion | bytes 49216 | tf_op jit(solution)/shard_map/scatter | solution.py:58
  114.5 5.5 %all-to-all-done.3 = f32[32,16,256]{2,1,0:T(8,128)} async-done(((f32[32,16,256]{2,1,0:T(8,128)}), f32[32,16,256]{2,1,0:T(8,128)}, u32[]{:S(2)}, u32[]{:S(2)}) %all-to-all-start.3) | async-done | bytes 524320 | tf_op jit(solution)/shard_map/all_to_all | solution.py:10
  119.9 1.9 %copy.21 = f32[512,256]{1,0:T(8,128)} copy(f32[512,256]{1,0:T(8,128)} %bitcast.8) | data formatting | bytes 1048576
  (27 shorter events, 1.0 us)
Async XLA Ops:
  0.6 14.4 %all-to-all-start = ((s32[32,1,64]{2,1,0:T(1,128)}), s32[32,1,64]{2,1,0:T(1,128)S(1)}, u32[]{:S(2)}, u32[]{:S(2)}) async-start(s32[32,1,64]{2,1,0:T(1,128)} %bitcast.23), calls=%async_computation | async-start | bytes 32768 | tf_op jit(solution)/shard_map/all_to_all | solution.py:10
  23.9 4.5 %copy-start.2 = (s32[1,32,64]{2,1,0:T(8,128)S(1)}, s32[1,32,64]{2,1,0:T(8,128)}, u32[]{:S(2)}) copy-start(s32[1,32,64]{2,1,0:T(8,128)} %param.10) | copy-start | bytes 24580
  23.9 4.6 %copy-start.3 = (s32[256,8]{0,1:T(8,128)S(1)}, s32[256,8]{0,1:T(8,128)}, u32[]{:S(2)}) copy-start(s32[256,8]{0,1:T(8,128)} %param.11) | copy-start | bytes 24580
  23.9 4.7 %copy-start.1 = (f32[256,256]{1,0:T(8,128)S(1)}, f32[256,256]{1,0:T(8,128)}, u32[]{:S(2)}) copy-start(f32[256,256]{1,0:T(8,128)} %param.12) | copy-start | bytes 786436
  25.1 35.2 %all-to-all-start.1 = ((bf16[32,80,256]{2,1,0:T(8,128)(2,1)}), bf16[32,80,256]{2,1,0:T(8,128)(2,1)S(1)}, u32[]{:S(2)}, u32[]{:S(2)}) async-start(bf16[32,80,256]{2,1,0:T(8,128)(2,1)} %pad_maximum_fusion), calls=%async_computation.1 | async-start | bytes 2621440 | tf_op jit(solution)/shard_map/all_to_all | solution.py:10
  60.5 1.7 %copy-start.4 = (s32[256]{0:T(256)S(1)}, s32[256]{0:T(256)}, u32[]{:S(2)}) copy-start(s32[256]{0:T(256)} %param.13) | copy-start | bytes 3076
  100.2 6.2 %copy-start = (f32[2048,256]{1,0:T(8,128)S(1)}, f32[2048,256]{1,0:T(8,128)}, u32[]{:S(2)}) copy-start(f32[2048,256]{1,0:T(8,128)} %param.7) | copy-start | bytes 6291460
  101.0 18.9 %all-to-all-start.3 = ((f32[32,16,256]{2,1,0:T(8,128)}), f32[32,16,256]{2,1,0:T(8,128)}, u32[]{:S(2)}, u32[]{:S(2)}) async-start(f32[32,16,256]{2,1,0:T(8,128)} %broadcast_in_dim.8), calls=%async_computation.3 | async-start | bytes 1048576 | tf_op jit(solution)/shard_map/all_to_all | solution.py:10

commit v2 on v1

--- a/solution.py
+++ b/solution.py
@@ -1,22 +1,415 @@
 import jax
 import jax.numpy as jnp
 from jax import lax
+from jax.experimental import pallas as pl
+from jax.experimental.pallas import tpu as pltpu
 from jax.sharding import PartitionSpec as P
 
+
 AXES = ("rows", "grp")
+LANES = 128
+MIB = 1 << 20
+BF16 = jnp.bfloat16
+F32 = jnp.float32
+I32 = jnp.int32
 
 
 def exchange(x):
     return lax.all_to_all(x, AXES, split_axis=0, concat_axis=0, tiled=True)
 
 
-def body(table, hot_slot, cold_row, cold_bag, hot_pick, dense, label):
+def column(row):
+    return jnp.transpose(jnp.broadcast_to(row, (LANES, LANES)))
+
+
+def lane_iota(shape):
+    return lax.broadcasted_iota(I32, shape, 1)
+
+
+def one_hot(mask):
+    return jnp.where(mask, 1.0, 0.0).astype(BF16)
+
+
+def packed_row(ref, at, per_peer, part):
+    row = None
+    for j in range(LANES // per_peer):
+        shift = (j - part) * per_peer % LANES
+        other = ref[at(j)]
+        other = pltpu.roll(other, shift, 1) if shift else other
+        row = other if row is None else jnp.where(lane_iota(row.shape) < j * per_peer, row, other)
+    return row
+
+
+def mark_of(ids):
+    return ((LANES + (ids & (LANES - 1))) << (ids >> 7)).astype(F32).astype(BF16)
+
+
+def fetch(pairs, sems):
+    copies = [pltpu.make_async_copy(a, b, sems.at[k]) for k, (a, b) in enumerate(pairs)]
+    for copy in copies:
+        copy.start()
+    return copies
+
+
+def offsets(chunks):
+    return [sum(chunk.shape[0] for chunk in chunks[:k]) for k in range(len(chunks))]
+
+
+def prepare_kernel(
+    slot_ref, table_hbm, dense_hbm, pick_hbm, packed_ref, hot_ref, dense_ref, pick_ref, sems
+):
+    own_hot = slot_ref.shape[0]
+    dense_in, pick_in, *rows_in = fetch(
+        [(dense_hbm, dense_ref), (pick_hbm, pick_ref)]
+        + [
+            (table_hbm.at[pl.ds(slot_ref[k], 1)], hot_ref.at[pl.ds(k, 1)])
+            for k in range(own_hot)
+        ],
+        sems,
+    )
+    samples = dense_ref.shape[0]
+    dense_in.wait()
+    packed_ref[:samples, :] = dense_ref[...].astype(BF16)
+    pick_in.wait()
+    packed_ref[samples + 2 * own_hot :, :] = mark_of(pick_ref[...])
+    for row_in in rows_in:
+        row_in.wait()
+    hot = hot_ref[...]
+    high = hot.astype(BF16)
+    packed_ref[samples : samples + own_hot, :] = high
+    packed_ref[samples + own_hot : samples + 2 * own_hot, :] = (hot - high.astype(F32)).astype(BF16)
+
+
+def lookup_kernel(request_ref, table_ref, out_ref):
+    peers = request_ref.shape[0]
+    rows = table_ref.shape[0]
+    per_peer = request_ref.shape[2] // 2
+    group = LANES // per_peer
+    tile = 4
+    table = table_ref[...].astype(BF16)
+    for first in range(0, peers // group, tile):
+        pieces = []
+        for k in range(first, first + tile):
+            wanted = column(packed_row(request_ref, lambda j: k * group + j, per_peer, 0))
+            pieces.append(
+                jnp.concatenate(
+                    [one_hot(wanted == lane_iota(wanted.shape) + c) for c in range(0, rows, LANES)],
+                    axis=1,
+                )
+            )
+        hits = jnp.concatenate(pieces, axis=0)
+        out_ref[first * LANES : (first + tile) * LANES, :] = jnp.dot(
+            hits, table, preferred_element_type=F32
+        ).astype(BF16)
+
+
+def marks_kernel(source_ref, me_ref, request_ref, *refs):
+    *chunks, hot_ref, cold_ref, pick_ref, sems = refs
+    per_peer = request_ref.shape[2] // 2
+    samples = cold_ref.shape[1]
+    own_hot = 2 * hot_ref.shape[0] // request_ref.shape[0]
+    first = samples + 2 * own_hot
+    picks_in = fetch(
+        [
+            (chunk.at[:, first:], pick_ref.at[pl.ds(n, chunk.shape[0])])
+            for n, chunk in zip(offsets(chunks), chunks)
+        ],
+        sems,
+    )
+    one, zero = jnp.ones((), BF16), jnp.zeros((), BF16)
+    for n in range(request_ref.shape[0]):
+        bags = column(request_ref[source_ref[n]])[per_peer:]
+        at = n * per_peer
+        for c in range(0, samples, LANES):
+            cold_ref[at : at + per_peer, c : c + LANES] = one_hot(bags == lane_iota(bags.shape) + c)
+    rows = lax.broadcasted_iota(I32, (hot_ref.shape[0], LANES), 0)
+    odd = me_ref[0] & 1
+    ids = mark_of(rows + (rows // own_hot + odd) * own_hot)
+    for arrived in picks_in:
+        arrived.wait()
+    for n in range(pick_ref.shape[0]):
+        for c in range(0, samples, LANES):
+            total = None
+            for j in range(pick_ref.shape[1]):
+                hit = jnp.where(ids == pick_ref[n, j : j + 1, c : c + LANES], one, zero)
+                total = hit if total is None else total + hit
+            at = n * samples + c
+            hot_ref[:, at : at + LANES] = total
+
+
+def pool_kernel(source_ref, rows_ref, bag_hbm, pick_hbm, dense_hbm, label_hbm, *refs):
+    *chunks, pooled_ref, err_ref, hot_ref, near_ref, bag_ref, pick_ref, dense_ref, label_ref, sems = refs
+    samples, width = dense_ref.shape
+    hot_total = hot_ref.shape[0]
+    own_hot = hot_total // err_ref.shape[0]
+    high = slice(samples, samples + own_hot)
+    bag_in, pick_in, dense_in, label_in, *hot_in = fetch(
+        [
+            (bag_hbm, bag_ref),
+            (pick_hbm, pick_ref),
+            (dense_hbm, dense_ref),
+            (label_hbm, label_ref),
+        ]
+        + [
+            (chunk.at[:, high], near_ref.at[pl.ds(n, chunk.shape[0])])
+            for n, chunk in zip(offsets(chunks), chunks)
+        ],
+        sems,
+    )
+    bag_in.wait()
+    ids = lax.broadcasted_iota(I32, (samples, LANES), 0)
+    chosen = jnp.concatenate(
+        [one_hot(ids == bag_ref[k : k + 1, :]) for k in range(bag_ref.shape[0])], axis=1
+    )
+    pooled = jnp.dot(chosen, rows_ref[...], preferred_element_type=F32)
+    pick_in.wait()
+    counts = []
+    for h in range(0, hot_total, LANES):
+        ids = lax.broadcasted_iota(I32, (LANES, samples), 0) + h
+        total = jnp.zeros((LANES, samples), F32)
+        for j in range(pick_ref.shape[0]):
+            total = total + jnp.where(ids == pick_ref[j : j + 1, :], 1.0, 0.0)
+        counts.append(total.astype(BF16))
+    for arrived in hot_in:
+        arrived.wait()
+    for n in range(near_ref.shape[0]):
+        at = pl.multiple_of(source_ref[n] * own_hot, own_hot)
+        hot_ref[pl.ds(at, own_hot), :] = near_ref[n]
+    pooled = pooled + lax.dot_general(
+        jnp.concatenate(counts, axis=0),
+        hot_ref[...],
+        (((0,), (0,)), ((), ())),
+        preferred_element_type=F32,
+    )
+    pooled_ref[...] = pooled
+    dense_in.wait()
+    label_in.wait()
+    score = jnp.sum(pooled * dense_ref[...], axis=1, keepdims=True) / width**0.5
+    flat = jnp.transpose(jnp.broadcast_to(score, (samples, LANES)))[:1, :]
+    err = 1.0 / (1.0 + jnp.exp(-flat)) - label_ref[...].astype(F32)
+    err_ref[...] = jnp.broadcast_to(err[None], err_ref.shape)
+
+
+def hot_kernel(source_ref, me_ref, marks_ref, err_ref, *refs):
+    *chunks, new_ref, grad_ref = refs
+    hot_half, _ = new_ref.shape
+    peers = err_ref.shape[0]
+    samples = err_ref.shape[2]
+    own_hot = 2 * hot_half // peers
+    total, n = None, 0
+    for chunk in chunks:
+        parts = chunk.shape[0]
+        errs = [err_ref[source_ref[n + p]].astype(BF16) for p in range(parts)]
+        near = jnp.dot(
+            marks_ref[:, n * samples : (n + parts) * samples] * jnp.concatenate(errs, axis=1),
+            jnp.concatenate([chunk[p, :samples, :] for p in range(parts)], axis=0),
+            preferred_element_type=F32,
+        )
+        total = near if total is None else total + near
+        n += parts
+    grad_ref[...] = total
+    odd = me_ref[0] & 1
+    n = 0
+    for chunk in chunks:
+        for p in range(chunk.shape[0]):
+            owner = source_ref[n]
+
+            @pl.when((owner & 1) == odd)
+            def _():
+                at = pl.multiple_of((owner // 2) * own_hot, own_hot)
+                old = chunk[p, samples : samples + own_hot, :].astype(F32)
+                old = old + chunk[p, samples + own_hot : samples + 2 * own_hot, :].astype(F32)
+                new_ref[pl.ds(at, own_hot), :] = old - 0.1 * grad_ref[pl.ds(at, own_hot), :]
+
+            n += 1
+
+
+def cold_kernel(
+    source_ref, slot_ref, me_ref, cold_ref, err_ref, request_ref, table_ref, hot_ref, *refs
+):
+    *chunks, new_ref, slots_ref = refs
+    rows = table_ref.shape[0]
+    peers = request_ref.shape[0]
+    samples = cold_ref.shape[1]
+    per_peer = request_ref.shape[2] // 2
+    own_hot = slot_ref.shape[0]
+    n = 0
+    for chunk in chunks:
+        for p in range(chunk.shape[0]):
+            at = n * per_peer
+            part = jnp.dot(
+                cold_ref[at : at + per_peer, :] * err_ref[source_ref[n]].astype(BF16),
+                chunk[p, :samples, :],
+                preferred_element_type=F32,
+            )
+            slots_ref[at : at + per_peer, :] = part.astype(BF16)
+            n += 1
+    group = LANES // per_peer
+    packed = [
+        packed_row(request_ref, lambda j: source_ref[n + j], per_peer, 0)
+        for n in range(0, peers, group)
+    ]
+    chunk_rows = 256
+    ids = lax.broadcasted_iota(I32, (chunk_rows, LANES), 0)
+    for r in range(0, rows, chunk_rows):
+        place = jnp.concatenate([one_hot(ids + r == row) for row in packed], axis=1)
+        moved = jnp.dot(place, slots_ref[...], preferred_element_type=F32)
+        new_ref[r : r + chunk_rows, :] = table_ref[r : r + chunk_rows, :] - 0.1 * moved
+    base = (me_ref[0] // 2) * own_hot
+    for k in range(own_hot):
+        new_ref[pl.ds(slot_ref[k], 1), :] = hot_ref[pl.ds(base + k, 1), :]
+
+
+def gather_all(x, devices):
+    def swap(held, mask):
+        return lax.ppermute(held, AXES, [(i, i ^ mask(i)) for i in range(devices)])
+
+    first = lambda i: 2 if i & 1 else 4
+    second = lambda i: 4 if i & 1 else 2
+    other = lambda i: 1
+    deep = [swap(x, lambda i: mask) for mask in deep_masks(devices)]
+    near = [x, swap(x, first), swap(x, second)]
+    near = jnp.concatenate(near + [swap(near[1], second)], axis=0)
+    own = jnp.concatenate(deep, axis=0)
+    across = swap(own, first)
+    up = swap(own, second)
+    held = [near, own, across, up, swap(across, second)]
+    return held + [swap(chunk, other) for chunk in held]
+
+
+def deep_masks(devices):
+    masks = [0]
+    for b in range(devices.bit_length() - 2, 2, -1):
+        masks += [mask | 1 << b for mask in masks]
+    return masks[1:]
+
+
+def sources_of(me, devices):
+    deep = deep_masks(devices)
+
+    def half(owner):
+        first = jnp.where(owner & 1 == 1, 2, 4)
+        turns = [0, first, 6 - first, 6]
+        return [owner ^ turn for turn in turns] + [owner ^ turn ^ m for turn in turns for m in deep]
+
+    return jnp.stack(half(me) + half(me ^ 1)).astype(I32)
+
+
+def gathered_body(table, hot_slot, cold_row, cold_bag, hot_pick, dense, label):
+    rows, width = table.shape
+    samples = dense.shape[0]
+    own_hot = hot_slot.shape[0]
+    peers, per_peer = cold_row.shape[1], cold_row.shape[2]
+    slots = peers * per_peer
+    hot_total = peers * own_hot
+    me = lax.axis_index(AXES).astype(I32)
+    source = sources_of(me, peers)
+
+    def shape(*dims, kind=BF16):
+        return jax.ShapeDtypeStruct(dims, kind)
+
+    def call(kernel, out_shape, where, inputs, mib, flops, scratch):
+        spaces = {"s": pltpu.SMEM, "v": pltpu.VMEM, "h": pltpu.HBM}
+        specs = [pl.BlockSpec(memory_space=spaces[w]) for w in where]
+        return pl.pallas_call(
+            kernel,
+            out_shape=out_shape,
+            in_specs=specs[: len(inputs)],
+            out_specs=tuple(specs[len(inputs) :]),
+            scratch_shapes=scratch,
+            compiler_params=pltpu.CompilerParams(vmem_limit_bytes=mib * MIB),
+            cost_estimate=pl.CostEstimate(flops=flops, bytes_accessed=4 * MIB, transcendentals=0),
+        )(*inputs)
+
+    def copies(count):
+        return pltpu.SemaphoreType.DMA((count,))
+
+    request = exchange(jnp.concatenate([cold_row[0], cold_bag[0]], axis=1)[:, None, :])
+    part_rows = samples + 2 * own_hot + hot_pick.shape[1]
+    work = slots * rows * width
+    picks = hot_pick.T
+    bags = cold_bag.reshape(slots // LANES, LANES)
+    (packed,) = call(
+        prepare_kernel,
+        (shape(part_rows, width),),
+        "shhhv",
+        [hot_slot, table, dense, picks],
+        63,
+        work,
+        [
+            pltpu.VMEM((own_hot, width), F32),
+            pltpu.VMEM((samples, width), F32),
+            pltpu.VMEM(picks.shape, I32),
+            copies(2 + own_hot),
+        ],
+    )
+    chunks = gather_all(packed[None], peers)
+    many = "v" * len(chunks)
+    (looked,) = call(
+        lookup_kernel, (shape(slots, width),), "vvv", [request, table], 24, 2 * work, []
+    )
+    returned = exchange(looked.reshape(peers, per_peer, width)).reshape(slots, width)
+    pooled, err = call(
+        pool_kernel,
+        (shape(samples, width, kind=F32), shape(peers, 1, samples, kind=F32)),
+        "svhhhh" + "h" * len(chunks) + "vv",
+        [source, returned, bags, picks, dense, label.reshape(1, samples)] + chunks,
+        24,
+        work,
+        [
+            pltpu.VMEM((hot_total, width), BF16),
+            pltpu.VMEM((peers, own_hot, width), BF16),
+            pltpu.VMEM(bags.shape, I32),
+            pltpu.VMEM(picks.shape, I32),
+            pltpu.VMEM((samples, width), F32),
+            pltpu.VMEM((1, samples), I32),
+            copies(4 + len(chunks)),
+        ],
+    )
+    errs = exchange(err)
+    marks, cold = call(
+        marks_kernel,
+        (shape(hot_total // 2, peers * samples), shape(slots, samples)),
+        "ssv" + "h" * len(chunks) + "vv",
+        [source, me[None], request] + chunks,
+        24,
+        4 * work,
+        [pltpu.VMEM((peers, hot_pick.shape[1], samples), BF16), copies(len(chunks))],
+    )
+    (hot_here,) = call(
+        hot_kernel,
+        (shape(hot_total // 2, width, kind=F32),),
+        "ssvv" + many + "v",
+        [source, me[None], marks, errs] + chunks,
+        24,
+        work,
+        [pltpu.VMEM((hot_total // 2, width), F32)],
+    )
+    hot_there = lax.ppermute(hot_here, AXES, [(i, i ^ 1) for i in range(peers)])
+    (new_table,) = call(
+        cold_kernel,
+        (shape(rows, width, kind=F32),),
+        "sssvvvvv" + many + "v",
+        [source, hot_slot, me[None], cold, errs, request, table, hot_here] + chunks,
+        24,
+        4 * work,
+        [pltpu.VMEM((slots, width), BF16)],
+    )
+    split = (peers // 2, 1, own_hot, width)
+    here, there = hot_here.reshape(split), hot_there.reshape(split)
+    odd = (me & 1) == 1
+    hot_new = jnp.concatenate([jnp.where(odd, there, here), jnp.where(odd, here, there)], axis=1)
+    hot_new = hot_new.reshape(hot_total, width)
+    return (pooled, new_table, hot_new)
+
+
+def exchanged_body(table, hot_slot, cold_row, cold_bag, hot_pick, dense, label):
     width = table.shape[1]
     samples = dense.shape[0]
     own_hot = hot_slot.shape[0]
     peers, per_peer = cold_row.shape[1], cold_row.shape[2]
     slots = peers * per_peer
-    bf16 = jnp.bfloat16
+    bf16 = BF16
     arrived = exchange(cold_row[0]).reshape(slots)
     rounded = table.astype(bf16)
     owned = jnp.arange(table.shape[0], dtype=jnp.int32)
@@ -70,6 +463,16 @@
         P(AXES, None),
         P(AXES),
     )
+    devices = mesh.shape["rows"] * mesh.shape["grp"]
+
+    def body(*blocks):
+        _, hot_slot, cold_row, _, _, dense, _ = blocks
+        samples, own_hot = dense.shape[0], hot_slot.shape[0]
+        marks = 2 * devices * samples * devices * own_hot
+        fits = marks <= 16 * MIB and 2 * cold_row.shape[2] == LANES
+        fits = fits and devices & (devices - 1) == 0 and devices >= 16 and devices * own_hot <= 64 * LANES
+        return (gathered_body if fits else exchanged_body)(*blocks)
+
     return jax.shard_map(
         body,
         mesh=mesh,

time: 122 us -> 123 us (level)
  Pallas kernels: 0 us -> 24.3 us
  blocking collectives: 36.6 us -> 14.3 us
  waiting for transfers between devices: 37.9 us -> 50.8 us
  local copies, waits for them, and re-layouts: 19 us -> 8.73 us
  starting transfers between devices: 14 us -> 21.7 us
  matrix products: 7.39 us -> 0 us
  other arithmetic: 6.06 us -> 1.87 us
    ppermute x0 -> x15, waiting for transfers between devices: none -> 50.8 us  [the longest x14 50.8 us: swap(): return lax.ppermute(held, AXES, [(i, i ^ mask(i)) for i in range(devices)])]
    all_to_all x3 -> x2, waiting for transfers between devices: 37.9 us -> 0.01 us  [exchange(): return lax.all_to_all(x, AXES, split_axis=0, concat_axis=0, tiled=True)]
    pallas_call x0 -> x6, Pallas kernels: none -> 24.3 us  [call(): pl.pallas_call(kernel, out_shape=out_shape, in_specs=specs[:len(inputs)],...]
    all_to_all x1, blocking collectives: 36.6 us -> 14.3 us  [exchange(): return lax.all_to_all(x, AXES, split_axis=0, concat_axis=0, tiled=True)]
    ppermute x0 -> x15, starting transfers between devices: none -> 13 us  [the longest x14 12.7 us: swap(): return lax.ppermute(held, AXES, [(i, i ^ mask(i)) for i in range(devices)])]
    gather x2 -> x0, local copies, waits for them, and re-layouts: 9.67 us -> none  [the longest x1 7.5 us: body(): looked = rounded[arrived].reshape(peers, per_peer, width)]
    dot_general x5 -> x0, matrix products: 7.39 us -> none  [the longest x1 4.58 us: body(): jnp.dot(placed, delivered[:, :per_peer].reshape(slots, width), preferred_...]
    all_to_all x3 -> x2, starting transfers between devices: 14 us -> 8.75 us  [exchange(): return lax.all_to_all(x, AXES, split_axis=0, concat_axis=0, tiled=True)]
  transfers between devices with their start and end apart: 3 -> 17, of which waited for: 3 -> 8; matrix products, arithmetic and copies ran while one was open for 14% -> 1% of each run, Pallas kernels for 0% -> 11%
where the time goes in v2:
time: 123 us
  waiting for transfers between devices  50.8 us (41%)
  Pallas kernels  24.3 us (20%)
  starting transfers between devices  21.7 us (18%)
  blocking collectives  14.3 us (12%)
  local copies, waits for them, and re-layouts  8.73 us (7%)
  other arithmetic  1.87 us (2%)
    ppermute x14, waiting for transfers between devices, swap(): return lax.ppermute(held, AXES, [(i, i ^ mask(i)) for i in range(devices)])  50.8 us
    pallas_call x6, Pallas kernels, call(): pl.pallas_call(kernel, out_shape=out_shape, in_specs=specs[:len(inputs)],...  24.3 us
    all_to_all x1, blocking collectives, exchange(): return lax.all_to_all(x, AXES, split_axis=0, concat_axis=0, tiled=True)  14.3 us
    ppermute x14, starting transfers between devices, swap(): return lax.ppermute(held, AXES, [(i, i ^ mask(i)) for i in range(devices)])  12.7 us
    all_to_all x2, starting transfers between devices, exchange(): return lax.all_to_all(x, AXES, split_axis=0, concat_axis=0, tiled=True)  8.75 us
    unnamed x24, local copies, waits for them, and re-layouts  7.7 us
  transfers between devices with their start and end apart: 17, of which 8 were waited for; matrix products, arithmetic and copies ran while one was open for 1% of the time, Pallas kernels for 11%

profile of v2, /device:TPU:0, one launch (start us, length us, event | category | flops | bytes accessed | tf_op | source)
XLA Modules:
  0.0 122.5 jit_solution(5250854482455728655)
XLA Ops:
  1.4 14.3 %all_to_all.15.request_ref = s32[32,1,128]{2,1,0:T(1,128)S(1)} all-to-all(s32[32,1,128]{2,1,0:T(1,128)S(1)} %bitcast.56), channel_id=1, replica_groups=mesh['rows'=8,'grp'=4] {'rows','grp'}, dimensions={0} | all-to-all | bytes 32768 | tf_op jit(solution)/shard_map/all_to_all | solution.py:18
  15.7 1.6 %copy-done.5 = f32[2048,256]{1,0:T(8,128)S(1)} copy-done((f32[2048,256]{1,0:T(8,128)S(1)}, f32[2048,256]{1,0:T(8,128)}, u32[]{:S(2)}) %copy-start.5) | copy-done | bytes 2097176
  17.3 3.4 %shard_map.94 = bf16[2048,256]{1,0:T(8,128)(2,1)} custom-call(s32[32,1,128]{2,1,0:T(1,128)S(1)} %all_to_all.15.request_ref, f32[2048,256]{1,0:T(8,128)S(1)} %copy-done.5), custom_call_target="tpu_custom_call" | custom-call | flops 2147483648 | bytes 4194304 | tf_op jit(solution)/shard_map/pallas_call | solution.py:314
  20.8 3.4 %all-to-all-start.1 = ((bf16[32,64,256]{2,1,0:T(8,128)(2,1)}), bf16[32,64,256]{2,1,0:T(8,128)(2,1)}, u32[]{:S(2)}, u32[]{:S(2)}) async-start(bf16[32,64,256]{2,1,0:T(8,128)(2,1)} %bitcast.35), calls=%async_computation.1 | async-start | bytes 2097152 | tf_op jit(solution)/shard_map/all_to_all | solution.py:18
  24.2 2.5 %shard_map.95 = bf16[296,256]{1,0:T(8,128)(2,1)} custom-call(s32[16]{0:T(128)} %slot_ref.3, f32[2048,256]{1,0:T(8,128)} %table_ref.3, f32[256,256]{1,0:T(8,128)} %dense_hbm.3, s32[8,256]{1,0:T(8,128)} %bitcast.43), custom_call_target="tpu_custom_call" | custom-call | flops 1073741824 | bytes 4194304 | tf_op jit(solution)/shard_map/pallas_call | solution.py:314
  26.7 2.6 %collective-permute-start.3 = (bf16[1,296,256]{2,1,0:T(8,128)(2,1)}, bf16[1,296,256]{2,1,0:T(8,128)(2,1)S(1)}, u32[]{:S(2)}, u32[]{:S(2)}) collective-permute-start(bf16[1,296,256]{2,1,0:T(8,128)(2,1)} %bitcast.49), channel_id=1, source_target_pairs={{0,16},{1,17},{2,18},{3,19},{4,20},{5,21},{6,22},{7,23},{8,24},{9,... | collective-permute-start | bytes 454664 | tf_op jit(solution)/shard_map/ppermute | solution.py:265
  29.3 1.5 %collective-permute-start.4 = (bf16[1,296,256]{2,1,0:T(8,128)(2,1)}, bf16[1,296,256]{2,1,0:T(8,128)(2,1)S(1)}, u32[]{:S(2)}, u32[]{:S(2)}) collective-permute-start(bf16[1,296,256]{2,1,0:T(8,128)(2,1)} %bitcast.50), channel_id=1, source_target_pairs={{0,8},{1,9},{2,10},{3,11},{4,12},{5,13},{6,14},{7,15},{8,0},{9,1},... | collective-permute-start | bytes 454664 | tf_op jit(solution)/shard_map/ppermute | solution.py:265
  31.1 29.4 %collective-permute-done.3 = bf16[1,296,256]{2,1,0:T(8,128)(2,1)S(1)} collective-permute-done((bf16[1,296,256]{2,1,0:T(8,128)(2,1)}, bf16[1,296,256]{2,1,0:T(8,128)(2,1)S(1)}, u32[]{:S(2)}, u32[]{:S(2)}) %collective-permute-start.3) | collective-permute-done | bytes 151584 | tf_op jit(solution)/shard_map/ppermute | solution.py:265
  60.6 1.6 %collective-permute-start.6 = (bf16[3,296,256]{2,1,0:T(8,128)(2,1)S(1)}, bf16[3,296,256]{2,1,0:T(8,128)(2,1)S(1)}, u32[]{:S(2)}, u32[]{:S(2)}) collective-permute-start(bf16[3,296,256]{2,1,0:T(8,128)(2,1)S(1)} %constant_dynamic-update-slice_fusion.refs_1_), channel_id=1, source_target_pairs={{0,4},{1,3},{2,6},{3,1},{4,0},{5,7},{6,2},{7,5},{8,12},{9,11},{10,... | collective-permute-start | bytes 1363976 | tf_op jit(solution)/shard_map/ppermute | solution.py:265
  62.7 1.5 %collective-permute-start.7 = (bf16[3,296,256]{2,1,0:T(8,128)(2,1)S(1)}, bf16[3,296,256]{2,1,0:T(8,128)(2,1)S(1)}, u32[]{:S(2)}, u32[]{:S(2)}) collective-permute-start(bf16[3,296,256]{2,1,0:T(8,128)(2,1)S(1)} %constant_dynamic-update-slice_fusion.refs_1_), channel_id=1, source_target_pairs={{0,2},{1,5},{2,0},{3,7},{4,6},{5,1},{6,4},{7,3},{8,10},{9,13},{10,... | collective-permute-start | bytes 1363976 | tf_op jit(solution)/shard_map/ppermute | solution.py:265
  64.2 9.8 %collective-permute-done.6.refs_2_ = bf16[3,296,256]{2,1,0:T(8,128)(2,1)S(1)} collective-permute-done((bf16[3,296,256]{2,1,0:T(8,128)(2,1)S(1)}, bf16[3,296,256]{2,1,0:T(8,128)(2,1)S(1)}, u32[]{:S(2)}, u32[]{:S(2)}) %collective-permute-start.6) | collective-permute-done | bytes 454688 | tf_op jit(solution)/shard_map/ppermute | solution.py:265
  74.0 1.5 %collective-permute-start.8 = (bf16[3,296,256]{2,1,0:T(8,128)(2,1)S(1)}, bf16[3,296,256]{2,1,0:T(8,128)(2,1)S(1)}, u32[]{:S(2)}, u32[]{:S(2)}) collective-permute-start(bf16[3,296,256]{2,1,0:T(8,128)(2,1)S(1)} %collective-permute-done.6.refs_2_), channel_id=1, source_target_pairs={{0,2},{1,5},{2,0},{3,7},{4,6},{5,1},{6,4},{7,3},{8,10},{9,13},{10,... | collective-permute-start | bytes 1363976 | tf_op jit(solution)/shard_map/ppermute | solution.py:265
  77.2 1.5 %collective-permute-start.2 = (bf16[1,296,256]{2,1,0:T(8,128)(2,1)S(1)}, bf16[1,296,256]{2,1,0:T(8,128)(2,1)S(1)}, u32[]{:S(2)}, u32[]{:S(2)}) collective-permute-start(bf16[1,296,256]{2,1,0:T(8,128)(2,1)S(1)} %collective-permute-done), channel_id=1, source_target_pairs={{0,2},{1,5},{2,0},{3,7},{4,6},{5,1},{6,4},{7,3},{8,10},{9,13},{10,... | collective-permute-start | bytes 454664 | tf_op jit(solution)/shard_map/ppermute | solution.py:265
  78.7 5.3 %collective-permute-done.1 = bf16[1,296,256]{2,1,0:T(8,128)(2,1)S(1)} collective-permute-done((bf16[1,296,256]{2,1,0:T(8,128)(2,1)}, bf16[1,296,256]{2,1,0:T(8,128)(2,1)S(1)}, u32[]{:S(2)}, u32[]{:S(2)}) %collective-permute-start.1) | collective-permute-done | bytes 151584 | tf_op jit(solution)/shard_map/ppermute | solution.py:265
  84.0 1.6 %collective-permute-done.2 = bf16[1,296,256]{2,1,0:T(8,128)(2,1)S(1)} collective-permute-done((bf16[1,296,256]{2,1,0:T(8,128)(2,1)S(1)}, bf16[1,296,256]{2,1,0:T(8,128)(2,1)S(1)}, u32[]{:S(2)}, u32[]{:S(2)}) %collective-permute-start.2) | collective-permute-done | bytes 151584 | tf_op jit(solution)/shard_map/ppermute | solution.py:265
  88.0 1.4 %collective-permute-done.10.refs_6_ = bf16[3,296,256]{2,1,0:T(8,128)(2,1)S(1)} collective-permute-done((bf16[3,296,256]{2,1,0:T(8,128)(2,1)S(1)}, bf16[3,296,256]{2,1,0:T(8,128)(2,1)S(1)}, u32[]{:S(2)}, u32[]{:S(2)}) %collective-permute-start.10) | collective-permute-done | bytes 454688 | tf_op jit(solution)/shard_map/ppermute | solution.py:265
  89.4 1.4 %collective-permute-done.12.refs_8_ = bf16[3,296,256]{2,1,0:T(8,128)(2,1)} collective-permute-done((bf16[3,296,256]{2,1,0:T(8,128)(2,1)S(1)}, bf16[3,296,256]{2,1,0:T(8,128)(2,1)}, u32[]{:S(2)}, u32[]{:S(2)}) %collective-permute-start.12) | collective-permute-done | bytes 454688 | tf_op jit(solution)/shard_map/ppermute | solution.py:265
  92.4 3.8 %shard_map.96 = (f32[256,256]{1,0:T(8,128)}, f32[32,1,256]{2,1,0:T(1,128)}) custom-call(s32[32]{0:T(128)S(1)} %stack.131.source_ref, bf16[2048,256]{1,0:T(8,128)(2,1)} %bitcast.36.rows_ref, s32[16,128]{1,0:T(8,128)S(1)} %reshape.69.bag_hbm, s32[8,256]{1,0:T(8,128)S(1)} %bitcast.44, f32[256,256]{1,0:T(8,128)S(1)} %copy-done.2, s32[1,256]{1,0:T(1,128)S(1)} %bitcast.45, ...), custom_call_target="tpu_custom_call" | custom-call | flops 1073741824 | bytes 4194304 | tf_op jit(solution)/shard_map/pallas_call | solution.py:314
  96.2 5.4 %all-to-all-start.2 = ((f32[32,1,256]{2,1,0:T(1,128)}), f32[32,1,256]{2,1,0:T(1,128)S(1)}, u32[]{:S(2)}, u32[]{:S(2)}) async-start(f32[32,1,256]{2,1,0:T(1,128)} %get-tuple-element.9), calls=%async_computation.2 | async-start | bytes 65536 | tf_op jit(solution)/shard_map/all_to_all | solution.py:18
  101.6 5.5 %shard_map.97 = (bf16[256,8192]{1,0:T(8,128)(2,1)S(1)}, bf16[2048,256]{1,0:T(8,128)(2,1)S(1)}) custom-call(s32[32]{0:T(128)S(1)} %stack.131.source_ref, s32[1]{0:T(128)} %bitcast.me_ref, s32[32,1,128]{2,1,0:T(1,128)S(1)} %all_to_all.15.request_ref, bf16[4,296,256]{2,1,0:T(8,128)(2,1)S(1)} %pad_maximum_fusion.refs_0_, ...), custom_call_target="tpu_custom_call" | custom-call | flops 4294967296 | bytes 4194304 | tf_op jit(solution)/shard_map/pallas_call | solution.py:314
  107.1 2.0 %copy-done = bf16[256,8192]{1,0:T(8,128)(2,1)} copy-done((bf16[256,8192]{1,0:T(8,128)(2,1)}, bf16[256,8192]{1,0:T(8,128)(2,1)S(1)}, u32[]{:S(2)}) %copy-start) | copy-done | bytes 4194328
  110.0 2.2 %copy-done.1 = bf16[256,8192]{1,0:T(8,128)(2,1)S(1)} copy-done((bf16[256,8192]{1,0:T(8,128)(2,1)S(1)}, bf16[256,8192]{1,0:T(8,128)(2,1)}, u32[]{:S(2)}) %copy-start.1) | copy-done | bytes 4194328
  112.2 3.4 %shard_map.98.hot_ref = f32[256,256]{1,0:T(8,128)S(1)} custom-call(s32[32]{0:T(128)S(1)} %stack.131.source_ref, s32[1]{0:T(128)} %bitcast.me_ref, bf16[256,8192]{1,0:T(8,128)(2,1)S(1)} %copy-done.1, f32[32,1,256]{2,1,0:T(1,128)S(1)} %all-to-all-done.2.err_ref, bf16[4,296,256]{2,1,0:T(8,128)(2,1)S(1)} %pad_maximum_fusion.refs_0_, ...), custom_call_target="tpu_custom_call" | custom-call | flops 1073741824 | bytes 4194304 | tf_op jit(solution)/shard_map/pallas_call | solution.py:314
  115.9 5.7 %shard_map.99 = f32[2048,256]{1,0:T(8,128)} custom-call(s32[32]{0:T(128)S(1)} %stack.131.source_ref, s32[16]{0:T(128)S(1)} %copy-done.7, s32[1]{0:T(128)} %bitcast.me_ref, bf16[2048,256]{1,0:T(8,128)(2,1)S(1)} %copy-done.9, f32[32,1,256]{2,1,0:T(1,128)S(1)} %all-to-all-done.2.err_ref, s32[32,1,128]{2,1,0:T(1,128)S(1)} %all_to_all.15.request_ref, ...), custom_call_target="tpu_custom_call" | custom-call | flops 4294967296 | bytes 4194304 | tf_op jit(solution)/shard_map/pallas_call | solution.py:314
  (49 shorter events, 9.6 us)
Async XLA Ops:
  20.8 70.7 %all-to-all-start.1 = ((bf16[32,64,256]{2,1,0:T(8,128)(2,1)}), bf16[32,64,256]{2,1,0:T(8,128)(2,1)}, u32[]{:S(2)}, u32[]{:S(2)}) async-start(bf16[32,64,256]{2,1,0:T(8,128)(2,1)} %bitcast.35), calls=%async_computation.1 | async-start | bytes 2097152 | tf_op jit(solution)/shard_map/all_to_all | solution.py:18
  26.7 61.2 %copy-start.10 = (s32[1,32,64]{2,1,0:T(8,128)S(1)}, s32[1,32,64]{2,1,0:T(8,128)}, u32[]{:S(2)}) copy-start(s32[1,32,64]{2,1,0:T(8,128)} %param.10) | copy-start | bytes 24580
  26.7 64.8 %copy-start.3 = (s32[256,8]{0,1:T(8,128)S(1)}, s32[256,8]{0,1:T(8,128)}, u32[]{:S(2)}) copy-start(s32[256,8]{0,1:T(8,128)} %param.11) | copy-start | bytes 24580
  26.7 64.8 %copy-start.4 = (s32[256]{0:T(256)S(1)}, s32[256]{0:T(256)}, u32[]{:S(2)}) copy-start(s32[256]{0:T(256)} %param.13) | copy-start | bytes 3076
  26.7 33.8 %collective-permute-start.3 = (bf16[1,296,256]{2,1,0:T(8,128)(2,1)}, bf16[1,296,256]{2,1,0:T(8,128)(2,1)S(1)}, u32[]{:S(2)}, u32[]{:S(2)}) collective-permute-start(bf16[1,296,256]{2,1,0:T(8,128)(2,1)} %bitcast.49), channel_id=1, source_target_pairs={{0,16},{1,17},{2,18},{3,19},{4,20},{5,21},{6,22},{7,23},{8,24},{9,... | collective-permute-start | bytes 454664 | tf_op jit(solution)/shard_map/ppermute | solution.py:265
  29.3 31.2 %collective-permute-start.4 = (bf16[1,296,256]{2,1,0:T(8,128)(2,1)}, bf16[1,296,256]{2,1,0:T(8,128)(2,1)S(1)}, u32[]{:S(2)}, u32[]{:S(2)}) collective-permute-start(bf16[1,296,256]{2,1,0:T(8,128)(2,1)} %bitcast.50), channel_id=1, source_target_pairs={{0,8},{1,9},{2,10},{3,11},{4,12},{5,13},{6,14},{7,15},{8,0},{9,1},... | collective-permute-start | bytes 454664 | tf_op jit(solution)/shard_map/ppermute | solution.py:265
  30.9 29.7 %collective-permute-start.5 = (bf16[1,296,256]{2,1,0:T(8,128)(2,1)}, bf16[1,296,256]{2,1,0:T(8,128)(2,1)S(1)}, u32[]{:S(2)}, u32[]{:S(2)}) collective-permute-start(bf16[1,296,256]{2,1,0:T(8,128)(2,1)} %bitcast.51), channel_id=1, source_target_pairs={{0,24},{1,25},{2,26},{3,27},{4,28},{5,29},{6,30},{7,31},{8,16},{9,... | collective-permute-start | bytes 454664 | tf_op jit(solution)/shard_map/ppermute | solution.py:265
  60.6 13.4 %collective-permute-start.6 = (bf16[3,296,256]{2,1,0:T(8,128)(2,1)S(1)}, bf16[3,296,256]{2,1,0:T(8,128)(2,1)S(1)}, u32[]{:S(2)}, u32[]{:S(2)}) collective-permute-start(bf16[3,296,256]{2,1,0:T(8,128)(2,1)S(1)} %constant_dynamic-update-slice_fusion.refs_1_), channel_id=1, source_target_pairs={{0,4},{1,3},{2,6},{3,1},{4,0},{5,7},{6,2},{7,5},{8,12},{9,11},{10,... | collective-permute-start | bytes 1363976 | tf_op jit(solution)/shard_map/ppermute | solution.py:265
  62.2 15.1 %collective-permute-start = (bf16[1,296,256]{2,1,0:T(8,128)(2,1)}, bf16[1,296,256]{2,1,0:T(8,128)(2,1)S(1)}, u32[]{:S(2)}, u32[]{:S(2)}) collective-permute-start(bf16[1,296,256]{2,1,0:T(8,128)(2,1)} %bitcast.52), channel_id=1, source_target_pairs={{0,4},{1,3},{2,6},{3,1},{4,0},{5,7},{6,2},{7,5},{8,12},{9,11},{10,... | collective-permute-start | bytes 454664 | tf_op jit(solution)/shard_map/ppermute | solution.py:265
  62.7 24.6 %collective-permute-start.7 = (bf16[3,296,256]{2,1,0:T(8,128)(2,1)S(1)}, bf16[3,296,256]{2,1,0:T(8,128)(2,1)S(1)}, u32[]{:S(2)}, u32[]{:S(2)}) collective-permute-start(bf16[3,296,256]{2,1,0:T(8,128)(2,1)S(1)} %constant_dynamic-update-slice_fusion.refs_1_), channel_id=1, source_target_pairs={{0,2},{1,5},{2,0},{3,7},{4,6},{5,1},{6,4},{7,3},{8,10},{9,13},{10,... | collective-permute-start | bytes 1363976 | tf_op jit(solution)/shard_map/ppermute | solution.py:265
  74.0 13.8 %collective-permute-start.8 = (bf16[3,296,256]{2,1,0:T(8,128)(2,1)S(1)}, bf16[3,296,256]{2,1,0:T(8,128)(2,1)S(1)}, u32[]{:S(2)}, u32[]{:S(2)}) collective-permute-start(bf16[3,296,256]{2,1,0:T(8,128)(2,1)S(1)} %collective-permute-done.6.refs_2_), channel_id=1, source_target_pairs={{0,2},{1,5},{2,0},{3,7},{4,6},{5,1},{6,4},{7,3},{8,10},{9,13},{10,... | collective-permute-start | bytes 1363976 | tf_op jit(solution)/shard_map/ppermute | solution.py:265
  75.5 8.6 %collective-permute-start.1 = (bf16[1,296,256]{2,1,0:T(8,128)(2,1)}, bf16[1,296,256]{2,1,0:T(8,128)(2,1)S(1)}, u32[]{:S(2)}, u32[]{:S(2)}) collective-permute-start(bf16[1,296,256]{2,1,0:T(8,128)(2,1)} %bitcast.53), channel_id=1, source_target_pairs={{0,2},{1,5},{2,0},{3,7},{4,6},{5,1},{6,4},{7,3},{8,10},{9,13},{10,... | collective-permute-start | bytes 454664 | tf_op jit(solution)/shard_map/ppermute | solution.py:265
  77.2 8.4 %collective-permute-start.2 = (bf16[1,296,256]{2,1,0:T(8,128)(2,1)S(1)}, bf16[1,296,256]{2,1,0:T(8,128)(2,1)S(1)}, u32[]{:S(2)}, u32[]{:S(2)}) collective-permute-start(bf16[1,296,256]{2,1,0:T(8,128)(2,1)S(1)} %collective-permute-done), channel_id=1, source_target_pairs={{0,2},{1,5},{2,0},{3,7},{4,6},{5,1},{6,4},{7,3},{8,10},{9,13},{10,... | collective-permute-start | bytes 454664 | tf_op jit(solution)/shard_map/ppermute | solution.py:265
  86.6 2.7 %collective-permute-start.9 = (bf16[4,296,256]{2,1,0:T(8,128)(2,1)S(1)}, bf16[4,296,256]{2,1,0:T(8,128)(2,1)S(1)}, u32[]{:S(2)}, u32[]{:S(2)}) collective-permute-start(bf16[4,296,256]{2,1,0:T(8,128)(2,1)S(1)} %pad_maximum_fusion.refs_0_), channel_id=1, source_target_pairs={{0,1},{1,0},{2,3},{3,2},{4,5},{5,4},{6,7},{7,6},{8,9},{9,8},{10,11... | collective-permute-start | bytes 1818632 | tf_op jit(solution)/shard_map/ppermute | solution.py:265
  86.7 2.7 %collective-permute-start.10 = (bf16[3,296,256]{2,1,0:T(8,128)(2,1)S(1)}, bf16[3,296,256]{2,1,0:T(8,128)(2,1)S(1)}, u32[]{:S(2)}, u32[]{:S(2)}) collective-permute-start(bf16[3,296,256]{2,1,0:T(8,128)(2,1)S(1)} %constant_dynamic-update-slice_fusion.refs_1_), channel_id=1, source_target_pairs={{0,1},{1,0},{2,3},{3,2},{4,5},{5,4},{6,7},{7,6},{8,9},{9,8},{10,11... | collective-permute-start | bytes 1363976 | tf_op jit(solution)/shard_map/ppermute | solution.py:265
  87.2 3.6 %collective-permute-start.11 = (bf16[3,296,256]{2,1,0:T(8,128)(2,1)S(1)}, bf16[3,296,256]{2,1,0:T(8,128)(2,1)}, u32[]{:S(2)}, u32[]{:S(2)}) collective-permute-start(bf16[3,296,256]{2,1,0:T(8,128)(2,1)S(1)} %collective-permute-done.6.refs_2_), channel_id=1, source_target_pairs={{0,1},{1,0},{2,3},{3,2},{4,5},{5,4},{6,7},{7,6},{8,9},{9,8},{10,11... | collective-permute-start | bytes 1363976 | tf_op jit(solution)/shard_map/ppermute | solution.py:265
  87.3 3.5 %collective-permute-start.12 = (bf16[3,296,256]{2,1,0:T(8,128)(2,1)S(1)}, bf16[3,296,256]{2,1,0:T(8,128)(2,1)}, u32[]{:S(2)}, u32[]{:S(2)}) collective-permute-start(bf16[3,296,256]{2,1,0:T(8,128)(2,1)S(1)} %collective-permute-done.7.refs_3_), channel_id=1, source_target_pairs={{0,1},{1,0},{2,3},{3,2},{4,5},{5,4},{6,7},{7,6},{8,9},{9,8},{10,11... | collective-permute-start | bytes 1363976 | tf_op jit(solution)/shard_map/ppermute | solution.py:265
  87.7 3.7 %collective-permute-start.13 = (bf16[3,296,256]{2,1,0:T(8,128)(2,1)S(1)}, bf16[3,296,256]{2,1,0:T(8,128)(2,1)}, u32[]{:S(2)}, u32[]{:S(2)}) collective-permute-start(bf16[3,296,256]{2,1,0:T(8,128)(2,1)S(1)} %collective-permute-done.8.refs_4_), channel_id=1, source_target_pairs={{0,1},{1,0},{2,3},{3,2},{4,5},{5,4},{6,7},{7,6},{8,9},{9,8},{10,11... | collective-permute-start | bytes 1363976 | tf_op jit(solution)/shard_map/ppermute | solution.py:265
  96.2 13.8 %all-to-all-start.2 = ((f32[32,1,256]{2,1,0:T(1,128)}), f32[32,1,256]{2,1,0:T(1,128)S(1)}, u32[]{:S(2)}, u32[]{:S(2)}) async-start(f32[32,1,256]{2,1,0:T(1,128)} %get-tuple-element.9), calls=%async_computation.2 | async-start | bytes 65536 | tf_op jit(solution)/shard_map/all_to_all | solution.py:18
  110.0 2.2 %copy-start.1 = (bf16[256,8192]{1,0:T(8,128)(2,1)S(1)}, bf16[256,8192]{1,0:T(8,128)(2,1)}, u32[]{:S(2)}) copy-start(bf16[256,8192]{1,0:T(8,128)(2,1)} %copy-done) | copy-start | bytes 12582916
  112.2 3.7 %copy-start.6 = (f32[2048,256]{1,0:T(8,128)S(1)}, f32[2048,256]{1,0:T(8,128)}, u32[]{:S(2)}) copy-start(f32[2048,256]{1,0:T(8,128)} %table_ref.3) | copy-start | bytes 6291460
  112.2 3.7 %copy-start.7 = (s32[16]{0:T(128)S(1)}, s32[16]{0:T(128)}, u32[]{:S(2)}) copy-start(s32[16]{0:T(128)} %slot_ref.3) | copy-start | bytes 196
  112.2 3.7 %copy-start.9 = (bf16[2048,256]{1,0:T(8,128)(2,1)S(1)}, bf16[2048,256]{1,0:T(8,128)(2,1)}, u32[]{:S(2)}) copy-start(bf16[2048,256]{1,0:T(8,128)(2,1)} %copy-done.8) | copy-start | bytes 3145732
  115.6 6.1 %collective-permute-start.14 = (f32[256,256]{1,0:T(8,128)S(1)}, f32[256,256]{1,0:T(8,128)S(1)}, u32[]{:S(2)}, u32[]{:S(2)}) collective-permute-start(f32[256,256]{1,0:T(8,128)S(1)} %shard_map.98.hot_ref), channel_id=1, source_target_pairs={{0,1},{1,0},{2,3},{3,2},{4,5},{5,4},{6,7},{7,6},{8,9},{9,8},{10,11... | collective-permute-start | bytes 786440 | tf_op jit(solution)/shard_map/ppermute | solution.py:388
  (4 other events, 5.5 us)

commit v3 on v2

--- a/solution.py
+++ b/solution.py
@@ -104,7 +104,7 @@
 
 
 def marks_kernel(source_ref, me_ref, request_ref, *refs):
-    *chunks, hot_ref, cold_ref, pick_ref, sems = refs
+    *chunks, hot_ref, cold_ref, rows_ref, pick_ref, dense_ref, sems = refs
     per_peer = request_ref.shape[2] // 2
     samples = cold_ref.shape[1]
     own_hot = 2 * hot_ref.shape[0] // request_ref.shape[0]
@@ -116,8 +116,15 @@
         ],
         sems,
     )
+    dense_in = fetch(
+        [
+            (chunk.at[:, :samples], dense_ref.at[pl.ds(n, chunk.shape[0])])
+            for n, chunk in zip(offsets(chunks), chunks)
+        ],
+        sems.at[pl.ds(len(chunks), len(chunks))],
+    )
     one, zero = jnp.ones((), BF16), jnp.zeros((), BF16)
-    for n in range(request_ref.shape[0]):
+    for n in range(pick_ref.shape[0]):
         bags = column(request_ref[source_ref[n]])[per_peer:]
         at = n * per_peer
         for c in range(0, samples, LANES):
@@ -134,7 +141,14 @@
                 hit = jnp.where(ids == pick_ref[n, j : j + 1, c : c + LANES], one, zero)
                 total = hit if total is None else total + hit
             at = n * samples + c
-            hot_ref[:, at : at + LANES] = total
+            hot_ref[:, at : at + LANES] = total.astype(hot_ref.dtype)
+    for arrived in dense_in:
+        arrived.wait()
+    for n in range(pick_ref.shape[0]):
+        at = slice(n * per_peer, (n + 1) * per_peer)
+        rows_ref[at, :] = jnp.dot(
+            cold_ref[at, :], dense_ref[n], preferred_element_type=F32
+        ).astype(BF16)
 
 
 def pool_kernel(source_ref, rows_ref, bag_hbm, pick_hbm, dense_hbm, label_hbm, *refs):
@@ -190,7 +204,7 @@
     err_ref[...] = jnp.broadcast_to(err[None], err_ref.shape)
 
 
-def hot_kernel(source_ref, me_ref, marks_ref, err_ref, *refs):
+def hot_kernel(source_ref, me_ref, marks0_ref, marks1_ref, err_ref, *refs):
     *chunks, new_ref, grad_ref = refs
     hot_half, _ = new_ref.shape
     peers = err_ref.shape[0]
@@ -200,8 +214,11 @@
     for chunk in chunks:
         parts = chunk.shape[0]
         errs = [err_ref[source_ref[n + p]].astype(BF16) for p in range(parts)]
+        marks_ref, at = marks0_ref, n * samples
+        if at >= marks0_ref.shape[1]:
+            marks_ref, at = marks1_ref, at - marks0_ref.shape[1]
         near = jnp.dot(
-            marks_ref[:, n * samples : (n + parts) * samples] * jnp.concatenate(errs, axis=1),
+            marks_ref[:, at : at + parts * samples].astype(BF16) * jnp.concatenate(errs, axis=1),
             jnp.concatenate([chunk[p, :samples, :] for p in range(parts)], axis=0),
             preferred_element_type=F32,
         )
@@ -225,25 +242,23 @@
 
 
 def cold_kernel(
-    source_ref, slot_ref, me_ref, cold_ref, err_ref, request_ref, table_ref, hot_ref, *refs
+    source_ref, slot_ref, me_ref, cold0_ref, cold1_ref, rows0_ref, rows1_ref, err_ref, request_ref,
+    table_ref, hot_ref, new_ref, slots_ref,
 ):
-    *chunks, new_ref, slots_ref = refs
     rows = table_ref.shape[0]
     peers = request_ref.shape[0]
-    samples = cold_ref.shape[1]
     per_peer = request_ref.shape[2] // 2
     own_hot = slot_ref.shape[0]
-    n = 0
-    for chunk in chunks:
-        for p in range(chunk.shape[0]):
-            at = n * per_peer
-            part = jnp.dot(
-                cold_ref[at : at + per_peer, :] * err_ref[source_ref[n]].astype(BF16),
-                chunk[p, :samples, :],
-                preferred_element_type=F32,
-            )
-            slots_ref[at : at + per_peer, :] = part.astype(BF16)
-            n += 1
+    early = cold0_ref.shape[0] // per_peer
+    for n in range(peers):
+        cold_ref, rows_ref, at = cold0_ref, rows0_ref, n * per_peer
+        if n >= early:
+            cold_ref, rows_ref, at = cold1_ref, rows1_ref, (n - early) * per_peer
+        err = cold_ref[at : at + per_peer, :].astype(F32) * err_ref[source_ref[n]]
+        err = jnp.sum(err, axis=1, keepdims=True)
+        slots_ref[n * per_peer : (n + 1) * per_peer, :] = (
+            err * rows_ref[at : at + per_peer, :].astype(F32)
+        ).astype(BF16)
     group = LANES // per_peer
     packed = [
         packed_row(request_ref, lambda j: source_ref[n + j], per_peer, 0)
@@ -367,20 +382,36 @@
         ],
     )
     errs = exchange(err)
-    marks, cold = call(
-        marks_kernel,
-        (shape(hot_total // 2, peers * samples), shape(slots, samples)),
-        "ssv" + "h" * len(chunks) + "vv",
-        [source, me[None], request] + chunks,
-        24,
-        4 * work,
-        [pltpu.VMEM((peers, hot_pick.shape[1], samples), BF16), copies(len(chunks))],
-    )
+    early, depth = 4, hot_pick.shape[1]
+
+    def marks(group, order):
+        count = sum(chunk.shape[0] for chunk in group)
+        return call(
+            marks_kernel,
+            (
+                shape(hot_total // 2, count * samples, kind=jnp.float8_e4m3fn),
+                shape(count * per_peer, samples),
+                shape(count * per_peer, width),
+            ),
+            "ssv" + "h" * len(group) + "vvv",
+            [order, me[None], request] + group,
+            24,
+            count * hot_total * samples * depth,
+            [
+                pltpu.VMEM((count, depth, samples), BF16),
+                pltpu.VMEM((count, samples, width), BF16),
+                copies(2 * len(group)),
+            ],
+        )
+
+    ready = sum(chunk.shape[0] for chunk in chunks[:early])
+    marks0, cold0, rows0 = marks(chunks[:early], source[:ready])
+    marks1, cold1, rows1 = marks(chunks[early:], source[ready:])
     (hot_here,) = call(
         hot_kernel,
         (shape(hot_total // 2, width, kind=F32),),
-        "ssvv" + many + "v",
-        [source, me[None], marks, errs] + chunks,
+        "ssvvv" + many + "v",
+        [source, me[None], marks0, marks1, errs] + chunks,
         24,
         work,
         [pltpu.VMEM((hot_total // 2, width), F32)],
@@ -389,8 +420,10 @@
     (new_table,) = call(
         cold_kernel,
         (shape(rows, width, kind=F32),),
-        "sssvvvvv" + many + "v",
-        [source, hot_slot, me[None], cold, errs, request, table, hot_here] + chunks,
+        "sssvvvvvvvvv",
+        [
+            source, hot_slot, me[None], cold0, cold1, rows0, rows1, errs, request, table, hot_here,
+        ],
         24,
         4 * work,
         [pltpu.VMEM((slots, width), BF16)],

time: 123 us -> 126 us (1.024)
  local copies, waits for them, and re-layouts: 8.73 us -> 12 us
    unnamed x24 -> x42, local copies, waits for them, and re-layouts: 7.7 us -> 10.8 us
    pallas_call x6 -> x7, Pallas kernels: 24.3 us -> 24 us  [call(): pl.pallas_call(kernel, out_shape=out_shape, in_specs=specs[:len(inputs)],...]
  transfers between devices with their start and end apart: 17 -> 17, of which waited for: 8 -> 9; matrix products, arithmetic and copies ran while one was open for 1% -> 1% of each run, Pallas kernels for 11% -> 11%
where the time goes in v3:
time: 126 us
  waiting for transfers between devices  50.8 us (40%)
  Pallas kernels  24 us (19%)
  starting transfers between devices  21.7 us (17%)
  blocking collectives  14.3 us (11%)
  local copies, waits for them, and re-layouts  12 us (10%)
  other arithmetic  1.87 us (1%)
    ppermute x14, waiting for transfers between devices, swap(): return lax.ppermute(held, AXES, [(i, i ^ mask(i)) for i in range(devices)])  50.8 us
    pallas_call x7, Pallas kernels, call(): pl.pallas_call(kernel, out_shape=out_shape, in_specs=specs[:len(inputs)],...  24 us
    all_to_all x1, blocking collectives, exchange(): return lax.all_to_all(x, AXES, split_axis=0, concat_axis=0, tiled=True)  14.3 us
    ppermute x14, starting transfers between devices, swap(): return lax.ppermute(held, AXES, [(i, i ^ mask(i)) for i in range(devices)])  12.7 us
    unnamed x42, local copies, waits for them, and re-layouts  10.8 us
    all_to_all x2, starting transfers between devices, exchange(): return lax.all_to_all(x, AXES, split_axis=0, concat_axis=0, tiled=True)  8.91 us
  transfers between devices with their start and end apart: 17, of which 9 were waited for; matrix products, arithmetic and copies ran while one was open for 1% of the time, Pallas kernels for 11%

profile of v3, /device:TPU:0, one launch (start us, length us, event | category | flops | bytes accessed | tf_op | source)
XLA Modules:
  0.0 125.6 jit_solution(14636360397046487076)
XLA Ops:
  1.4 14.3 %all_to_all.15.request_ref = s32[32,1,128]{2,1,0:T(1,128)S(1)} all-to-all(s32[32,1,128]{2,1,0:T(1,128)S(1)} %bitcast.56), channel_id=1, replica_groups=mesh['rows'=8,'grp'=4] {'rows','grp'}, dimensions={0} | all-to-all | bytes 32768 | tf_op jit(solution)/shard_map/all_to_all | solution.py:18
  15.7 1.6 %copy-done.8 = f32[2048,256]{1,0:T(8,128)S(1)} copy-done((f32[2048,256]{1,0:T(8,128)S(1)}, f32[2048,256]{1,0:T(8,128)}, u32[]{:S(2)}) %copy-start.8) | copy-done | bytes 2097176
  17.3 3.4 %shard_map.94 = bf16[2048,256]{1,0:T(8,128)(2,1)} custom-call(s32[32,1,128]{2,1,0:T(1,128)S(1)} %all_to_all.15.request_ref, f32[2048,256]{1,0:T(8,128)S(1)} %copy-done.8), custom_call_target="tpu_custom_call" | custom-call | flops 2147483648 | bytes 4194304 | tf_op jit(solution)/shard_map/pallas_call | solution.py:329
  20.8 3.4 %all-to-all-start.1 = ((bf16[32,64,256]{2,1,0:T(8,128)(2,1)}), bf16[32,64,256]{2,1,0:T(8,128)(2,1)}, u32[]{:S(2)}, u32[]{:S(2)}) async-start(bf16[32,64,256]{2,1,0:T(8,128)(2,1)} %bitcast.35), calls=%async_computation.1 | async-start | bytes 2097152 | tf_op jit(solution)/shard_map/all_to_all | solution.py:18
  24.1 2.5 %shard_map.95 = bf16[296,256]{1,0:T(8,128)(2,1)} custom-call(s32[16]{0:T(128)} %slot_ref.3, f32[2048,256]{1,0:T(8,128)} %table_ref.3, f32[256,256]{1,0:T(8,128)} %dense_hbm.3, s32[8,256]{1,0:T(8,128)} %bitcast.43), custom_call_target="tpu_custom_call" | custom-call | flops 1073741824 | bytes 4194304 | tf_op jit(solution)/shard_map/pallas_call | solution.py:329
  26.7 2.6 %collective-permute-start.3 = (bf16[1,296,256]{2,1,0:T(8,128)(2,1)}, bf16[1,296,256]{2,1,0:T(8,128)(2,1)S(1)}, u32[]{:S(2)}, u32[]{:S(2)}) collective-permute-start(bf16[1,296,256]{2,1,0:T(8,128)(2,1)} %bitcast.49), channel_id=1, source_target_pairs={{0,16},{1,17},{2,18},{3,19},{4,20},{5,21},{6,22},{7,23},{8,24},{9,... | collective-permute-start | bytes 454664 | tf_op jit(solution)/shard_map/ppermute | solution.py:280
  29.3 1.5 %collective-permute-start.4 = (bf16[1,296,256]{2,1,0:T(8,128)(2,1)}, bf16[1,296,256]{2,1,0:T(8,128)(2,1)S(1)}, u32[]{:S(2)}, u32[]{:S(2)}) collective-permute-start(bf16[1,296,256]{2,1,0:T(8,128)(2,1)} %bitcast.50), channel_id=1, source_target_pairs={{0,8},{1,9},{2,10},{3,11},{4,12},{5,13},{6,14},{7,15},{8,0},{9,1},... | collective-permute-start | bytes 454664 | tf_op jit(solution)/shard_map/ppermute | solution.py:280
  31.1 29.4 %collective-permute-done.3 = bf16[1,296,256]{2,1,0:T(8,128)(2,1)S(1)} collective-permute-done((bf16[1,296,256]{2,1,0:T(8,128)(2,1)}, bf16[1,296,256]{2,1,0:T(8,128)(2,1)S(1)}, u32[]{:S(2)}, u32[]{:S(2)}) %collective-permute-start.3) | collective-permute-done | bytes 151584 | tf_op jit(solution)/shard_map/ppermute | solution.py:280
  60.6 1.6 %collective-permute-start.6 = (bf16[3,296,256]{2,1,0:T(8,128)(2,1)S(1)}, bf16[3,296,256]{2,1,0:T(8,128)(2,1)S(1)}, u32[]{:S(2)}, u32[]{:S(2)}) collective-permute-start(bf16[3,296,256]{2,1,0:T(8,128)(2,1)S(1)} %constant_dynamic-update-slice_fusion.refs_1_), channel_id=1, source_target_pairs={{0,4},{1,3},{2,6},{3,1},{4,0},{5,7},{6,2},{7,5},{8,12},{9,11},{10,... | collective-permute-start | bytes 1363976 | tf_op jit(solution)/shard_map/ppermute | solution.py:280
  62.7 1.5 %collective-permute-start.7 = (bf16[3,296,256]{2,1,0:T(8,128)(2,1)S(1)}, bf16[3,296,256]{2,1,0:T(8,128)(2,1)S(1)}, u32[]{:S(2)}, u32[]{:S(2)}) collective-permute-start(bf16[3,296,256]{2,1,0:T(8,128)(2,1)S(1)} %constant_dynamic-update-slice_fusion.refs_1_), channel_id=1, source_target_pairs={{0,2},{1,5},{2,0},{3,7},{4,6},{5,1},{6,4},{7,3},{8,10},{9,13},{10,... | collective-permute-start | bytes 1363976 | tf_op jit(solution)/shard_map/ppermute | solution.py:280
  64.2 9.8 %collective-permute-done.6.refs_2_ = bf16[3,296,256]{2,1,0:T(8,128)(2,1)S(1)} collective-permute-done((bf16[3,296,256]{2,1,0:T(8,128)(2,1)S(1)}, bf16[3,296,256]{2,1,0:T(8,128)(2,1)S(1)}, u32[]{:S(2)}, u32[]{:S(2)}) %collective-permute-start.6) | collective-permute-done | bytes 454688 | tf_op jit(solution)/shard_map/ppermute | solution.py:280
  74.0 1.5 %collective-permute-start.8 = (bf16[3,296,256]{2,1,0:T(8,128)(2,1)S(1)}, bf16[3,296,256]{2,1,0:T(8,128)(2,1)S(1)}, u32[]{:S(2)}, u32[]{:S(2)}) collective-permute-start(bf16[3,296,256]{2,1,0:T(8,128)(2,1)S(1)} %collective-permute-done.6.refs_2_), channel_id=1, source_target_pairs={{0,2},{1,5},{2,0},{3,7},{4,6},{5,1},{6,4},{7,3},{8,10},{9,13},{10,... | collective-permute-start | bytes 1363976 | tf_op jit(solution)/shard_map/ppermute | solution.py:280
  76.0 1.2 collective-permute-done
  77.2 1.5 %collective-permute-start.2 = (bf16[1,296,256]{2,1,0:T(8,128)(2,1)S(1)}, bf16[1,296,256]{2,1,0:T(8,128)(2,1)S(1)}, u32[]{:S(2)}, u32[]{:S(2)}) collective-permute-start(bf16[1,296,256]{2,1,0:T(8,128)(2,1)S(1)} %collective-permute-done), channel_id=1, source_target_pairs={{0,2},{1,5},{2,0},{3,7},{4,6},{5,1},{6,4},{7,3},{8,10},{9,13},{10,... | collective-permute-start | bytes 454664 | tf_op jit(solution)/shard_map/ppermute | solution.py:280
  78.7 5.3 %collective-permute-done.1 = bf16[1,296,256]{2,1,0:T(8,128)(2,1)S(1)} collective-permute-done((bf16[1,296,256]{2,1,0:T(8,128)(2,1)}, bf16[1,296,256]{2,1,0:T(8,128)(2,1)S(1)}, u32[]{:S(2)}, u32[]{:S(2)}) %collective-permute-start.1) | collective-permute-done | bytes 151584 | tf_op jit(solution)/shard_map/ppermute | solution.py:280
  84.0 1.6 %collective-permute-done.2 = bf16[1,296,256]{2,1,0:T(8,128)(2,1)S(1)} collective-permute-done((bf16[1,296,256]{2,1,0:T(8,128)(2,1)S(1)}, bf16[1,296,256]{2,1,0:T(8,128)(2,1)S(1)}, u32[]{:S(2)}, u32[]{:S(2)}) %collective-permute-start.2) | collective-permute-done | bytes 151584 | tf_op jit(solution)/shard_map/ppermute | solution.py:280
  88.0 1.4 %collective-permute-done.10.refs_6_.refs_2_ = bf16[3,296,256]{2,1,0:T(8,128)(2,1)S(1)} collective-permute-done((bf16[3,296,256]{2,1,0:T(8,128)(2,1)S(1)}, bf16[3,296,256]{2,1,0:T(8,128)(2,1)S(1)}, u32[]{:S(2)}, u32[]{:S(2)}) %collective-permute-start.10) | collective-permute-done | bytes 454688 | tf_op jit(solution)/shard_map/ppermute | solution.py:280
  92.4 3.7 %shard_map.96 = (f32[256,256]{1,0:T(8,128)}, f32[32,1,256]{2,1,0:T(1,128)S(1)}) custom-call(s32[32]{0:T(128)S(1)} %stack.136.source_ref, bf16[2048,256]{1,0:T(8,128)(2,1)} %bitcast.36.rows_ref, s32[16,128]{1,0:T(8,128)S(1)} %reshape.69.bag_hbm, s32[8,256]{1,0:T(8,128)S(1)} %bitcast.44, f32[256,256]{1,0:T(8,128)S(1)} %copy-done.4, s32[1,256]{1,0:T(1,128)S(1)} %bitcast.45, ...), custom_call_target="tpu_custom_call" | custom-call | flops 1073741824 | bytes 4194304 | tf_op jit(solution)/shard_map/pallas_call | solution.py:329
  96.7 5.5 %all-to-all-start.2 = ((f32[32,1,256]{2,1,0:T(1,128)}), f32[32,1,256]{2,1,0:T(1,128)S(1)}, u32[]{:S(2)}, u32[]{:S(2)}) async-start(f32[32,1,256]{2,1,0:T(1,128)} %copy-done.5), calls=%async_computation.2 | async-start | bytes 65536 | tf_op jit(solution)/shard_map/all_to_all | solution.py:18
  102.5 3.0 %shard_map.97 = (f8e4m3fn[256,3328]{1,0:T(32,128)(4,1)S(1)}, bf16[832,256]{1,0:T(8,128)(2,1)S(1)}, bf16[832,256]{1,0:T(8,128)(2,1)S(1)}) custom-call(s32[13]{0:T(128)S(1)} %stack.137.source_ref, s32[1]{0:T(128)} %bitcast.me_ref, s32[32,1,128]{2,1,0:T(1,128)S(1)} %all_to_all.15.request_ref, bf16[4,296,256]{2,1,0:T(8,128)(2,1)S(1)} %pad_maximum_fusion.refs_0_, ...), custom_call_target="tpu_custom_call" | custom-call | flops 13631488 | bytes 4194304 | tf_op jit(solution)/shard_map/pallas_call | solution.py:329
  107.9 4.0 %shard_map.98 = (f8e4m3fn[256,4864]{1,0:T(32,128)(4,1)S(1)}, bf16[1216,256]{1,0:T(8,128)(2,1)S(1)}, bf16[1216,256]{1,0:T(8,128)(2,1)S(1)}) custom-call(s32[19]{0:T(128)S(1)} %stack.138.source_ref, s32[1]{0:T(128)} %bitcast.me_ref, s32[32,1,128]{2,1,0:T(1,128)S(1)} %all_to_all.15.request_ref, bf16[3,296,256]{2,1,0:T(8,128)(2,1)S(1)} %collective-permute-done.8.refs_4_.refs_0_, ...), custom_call_target="tpu_custom_call" | custom-call | flops 19922944 | bytes 4194304 | tf_op jit(solution)/shard_map/pallas_call | solution.py:329
  114.6 1.3 %copy-done.1 = f8e4m3fn[256,4864]{1,0:T(32,128)(4,1)S(1)} copy-done((f8e4m3fn[256,4864]{1,0:T(32,128)(4,1)S(1)}, f8e4m3fn[256,4864]{1,0:T(32,128)(4,1)}, u32[]{:S(2)}) %copy-start.1) | copy-done | bytes 1245208
  117.0 3.1 %shard_map.99.hot_ref = f32[256,256]{1,0:T(8,128)S(1)} custom-call(s32[32]{0:T(128)S(1)} %stack.136.source_ref, s32[1]{0:T(128)} %bitcast.me_ref, f8e4m3fn[256,3328]{1,0:T(32,128)(4,1)S(1)} %copy-done.3, f8e4m3fn[256,4864]{1,0:T(32,128)(4,1)S(1)} %copy-done.1, f32[32,1,256]{2,1,0:T(1,128)S(1)} %all-to-all-done.2.err_ref, ...), custom_call_target="tpu_custom_call" | custom-call | flops 1073741824 | bytes 4194304 | tf_op jit(solution)/shard_map/pallas_call | solution.py:329
  120.4 4.3 %shard_map.100 = f32[2048,256]{1,0:T(8,128)} custom-call(s32[32]{0:T(128)S(1)} %stack.136.source_ref, s32[16]{0:T(128)S(1)} %copy-done.18, s32[1]{0:T(128)} %bitcast.me_ref, bf16[832,256]{1,0:T(8,128)(2,1)S(1)} %copy-done.15, bf16[1216,256]{1,0:T(8,128)(2,1)S(1)} %copy-done.11, bf16[832,256]{1,0:T(8,128)(2,1)S(1)} %copy-done.17, ...), custom_call_target="tpu_custom_call" | custom-call | flops 4294967296 | bytes 4194304 | tf_op jit(solution)/shard_map/pallas_call | solution.py:329
  (70 shorter events, 15.7 us)
Async XLA Ops:
  20.8 70.7 %all-to-all-start.1 = ((bf16[32,64,256]{2,1,0:T(8,128)(2,1)}), bf16[32,64,256]{2,1,0:T(8,128)(2,1)}, u32[]{:S(2)}, u32[]{:S(2)}) async-start(bf16[32,64,256]{2,1,0:T(8,128)(2,1)} %bitcast.35), calls=%async_computation.1 | async-start | bytes 2097152 | tf_op jit(solution)/shard_map/all_to_all | solution.py:18
  26.6 61.2 %copy-start.19 = (s32[1,32,64]{2,1,0:T(8,128)S(1)}, s32[1,32,64]{2,1,0:T(8,128)}, u32[]{:S(2)}) copy-start(s32[1,32,64]{2,1,0:T(8,128)} %param.10) | copy-start | bytes 24580
  26.7 64.8 %copy-start.6 = (s32[256,8]{0,1:T(8,128)S(1)}, s32[256,8]{0,1:T(8,128)}, u32[]{:S(2)}) copy-start(s32[256,8]{0,1:T(8,128)} %param.11) | copy-start | bytes 24580
  26.7 64.8 %copy-start.7 = (s32[256]{0:T(256)S(1)}, s32[256]{0:T(256)}, u32[]{:S(2)}) copy-start(s32[256]{0:T(256)} %param.13) | copy-start | bytes 3076
  26.7 33.8 %collective-permute-start.3 = (bf16[1,296,256]{2,1,0:T(8,128)(2,1)}, bf16[1,296,256]{2,1,0:T(8,128)(2,1)S(1)}, u32[]{:S(2)}, u32[]{:S(2)}) collective-permute-start(bf16[1,296,256]{2,1,0:T(8,128)(2,1)} %bitcast.49), channel_id=1, source_target_pairs={{0,16},{1,17},{2,18},{3,19},{4,20},{5,21},{6,22},{7,23},{8,24},{9,... | collective-permute-start | bytes 454664 | tf_op jit(solution)/shard_map/ppermute | solution.py:280
  29.3 31.2 %collective-permute-start.4 = (bf16[1,296,256]{2,1,0:T(8,128)(2,1)}, bf16[1,296,256]{2,1,0:T(8,128)(2,1)S(1)}, u32[]{:S(2)}, u32[]{:S(2)}) collective-permute-start(bf16[1,296,256]{2,1,0:T(8,128)(2,1)} %bitcast.50), channel_id=1, source_target_pairs={{0,8},{1,9},{2,10},{3,11},{4,12},{5,13},{6,14},{7,15},{8,0},{9,1},... | collective-permute-start | bytes 454664 | tf_op jit(solution)/shard_map/ppermute | solution.py:280
  30.9 29.7 %collective-permute-start.5 = (bf16[1,296,256]{2,1,0:T(8,128)(2,1)}, bf16[1,296,256]{2,1,0:T(8,128)(2,1)S(1)}, u32[]{:S(2)}, u32[]{:S(2)}) collective-permute-start(bf16[1,296,256]{2,1,0:T(8,128)(2,1)} %bitcast.51), channel_id=1, source_target_pairs={{0,24},{1,25},{2,26},{3,27},{4,28},{5,29},{6,30},{7,31},{8,16},{9,... | collective-permute-start | bytes 454664 | tf_op jit(solution)/shard_map/ppermute | solution.py:280
  60.6 13.4 %collective-permute-start.6 = (bf16[3,296,256]{2,1,0:T(8,128)(2,1)S(1)}, bf16[3,296,256]{2,1,0:T(8,128)(2,1)S(1)}, u32[]{:S(2)}, u32[]{:S(2)}) collective-permute-start(bf16[3,296,256]{2,1,0:T(8,128)(2,1)S(1)} %constant_dynamic-update-slice_fusion.refs_1_), channel_id=1, source_target_pairs={{0,4},{1,3},{2,6},{3,1},{4,0},{5,7},{6,2},{7,5},{8,12},{9,11},{10,... | collective-permute-start | bytes 1363976 | tf_op jit(solution)/shard_map/ppermute | solution.py:280
  62.2 15.1 %collective-permute-start = (bf16[1,296,256]{2,1,0:T(8,128)(2,1)}, bf16[1,296,256]{2,1,0:T(8,128)(2,1)S(1)}, u32[]{:S(2)}, u32[]{:S(2)}) collective-permute-start(bf16[1,296,256]{2,1,0:T(8,128)(2,1)} %bitcast.52), channel_id=1, source_target_pairs={{0,4},{1,3},{2,6},{3,1},{4,0},{5,7},{6,2},{7,5},{8,12},{9,11},{10,... | collective-permute-start | bytes 454664 | tf_op jit(solution)/shard_map/ppermute | solution.py:280
  62.7 24.6 %collective-permute-start.7 = (bf16[3,296,256]{2,1,0:T(8,128)(2,1)S(1)}, bf16[3,296,256]{2,1,0:T(8,128)(2,1)S(1)}, u32[]{:S(2)}, u32[]{:S(2)}) collective-permute-start(bf16[3,296,256]{2,1,0:T(8,128)(2,1)S(1)} %constant_dynamic-update-slice_fusion.refs_1_), channel_id=1, source_target_pairs={{0,2},{1,5},{2,0},{3,7},{4,6},{5,1},{6,4},{7,3},{8,10},{9,13},{10,... | collective-permute-start | bytes 1363976 | tf_op jit(solution)/shard_map/ppermute | solution.py:280
  74.0 13.8 %collective-permute-start.8 = (bf16[3,296,256]{2,1,0:T(8,128)(2,1)S(1)}, bf16[3,296,256]{2,1,0:T(8,128)(2,1)S(1)}, u32[]{:S(2)}, u32[]{:S(2)}) collective-permute-start(bf16[3,296,256]{2,1,0:T(8,128)(2,1)S(1)} %collective-permute-done.6.refs_2_), channel_id=1, source_target_pairs={{0,2},{1,5},{2,0},{3,7},{4,6},{5,1},{6,4},{7,3},{8,10},{9,13},{10,... | collective-permute-start | bytes 1363976 | tf_op jit(solution)/shard_map/ppermute | solution.py:280
  75.4 8.6 %collective-permute-start.1 = (bf16[1,296,256]{2,1,0:T(8,128)(2,1)}, bf16[1,296,256]{2,1,0:T(8,128)(2,1)S(1)}, u32[]{:S(2)}, u32[]{:S(2)}) collective-permute-start(bf16[1,296,256]{2,1,0:T(8,128)(2,1)} %bitcast.53), channel_id=1, source_target_pairs={{0,2},{1,5},{2,0},{3,7},{4,6},{5,1},{6,4},{7,3},{8,10},{9,13},{10,... | collective-permute-start | bytes 454664 | tf_op jit(solution)/shard_map/ppermute | solution.py:280
  77.2 8.4 %collective-permute-start.2 = (bf16[1,296,256]{2,1,0:T(8,128)(2,1)S(1)}, bf16[1,296,256]{2,1,0:T(8,128)(2,1)S(1)}, u32[]{:S(2)}, u32[]{:S(2)}) collective-permute-start(bf16[1,296,256]{2,1,0:T(8,128)(2,1)S(1)} %collective-permute-done), channel_id=1, source_target_pairs={{0,2},{1,5},{2,0},{3,7},{4,6},{5,1},{6,4},{7,3},{8,10},{9,13},{10,... | collective-permute-start | bytes 454664 | tf_op jit(solution)/shard_map/ppermute | solution.py:280
  86.6 2.7 %collective-permute-start.9 = (bf16[4,296,256]{2,1,0:T(8,128)(2,1)S(1)}, bf16[4,296,256]{2,1,0:T(8,128)(2,1)S(1)}, u32[]{:S(2)}, u32[]{:S(2)}) collective-permute-start(bf16[4,296,256]{2,1,0:T(8,128)(2,1)S(1)} %pad_maximum_fusion.refs_0_), channel_id=1, source_target_pairs={{0,1},{1,0},{2,3},{3,2},{4,5},{5,4},{6,7},{7,6},{8,9},{9,8},{10,11... | collective-permute-start | bytes 1818632 | tf_op jit(solution)/shard_map/ppermute | solution.py:280
  86.7 2.7 %collective-permute-start.10 = (bf16[3,296,256]{2,1,0:T(8,128)(2,1)S(1)}, bf16[3,296,256]{2,1,0:T(8,128)(2,1)S(1)}, u32[]{:S(2)}, u32[]{:S(2)}) collective-permute-start(bf16[3,296,256]{2,1,0:T(8,128)(2,1)S(1)} %constant_dynamic-update-slice_fusion.refs_1_), channel_id=1, source_target_pairs={{0,1},{1,0},{2,3},{3,2},{4,5},{5,4},{6,7},{7,6},{8,9},{9,8},{10,11... | collective-permute-start | bytes 1363976 | tf_op jit(solution)/shard_map/ppermute | solution.py:280
  87.2 2.9 %collective-permute-start.11 = (bf16[3,296,256]{2,1,0:T(8,128)(2,1)S(1)}, bf16[3,296,256]{2,1,0:T(8,128)(2,1)}, u32[]{:S(2)}, u32[]{:S(2)}) collective-permute-start(bf16[3,296,256]{2,1,0:T(8,128)(2,1)S(1)} %collective-permute-done.6.refs_2_), channel_id=1, source_target_pairs={{0,1},{1,0},{2,3},{3,2},{4,5},{5,4},{6,7},{7,6},{8,9},{9,8},{10,11... | collective-permute-start | bytes 1363976 | tf_op jit(solution)/shard_map/ppermute | solution.py:280
  87.3 3.5 %collective-permute-start.12 = (bf16[3,296,256]{2,1,0:T(8,128)(2,1)S(1)}, bf16[3,296,256]{2,1,0:T(8,128)(2,1)}, u32[]{:S(2)}, u32[]{:S(2)}) collective-permute-start(bf16[3,296,256]{2,1,0:T(8,128)(2,1)S(1)} %collective-permute-done.7.refs_3_), channel_id=1, source_target_pairs={{0,1},{1,0},{2,3},{3,2},{4,5},{5,4},{6,7},{7,6},{8,9},{9,8},{10,11... | collective-permute-start | bytes 1363976 | tf_op jit(solution)/shard_map/ppermute | solution.py:280
  87.7 3.7 %collective-permute-start.13 = (bf16[3,296,256]{2,1,0:T(8,128)(2,1)S(1)}, bf16[3,296,256]{2,1,0:T(8,128)(2,1)}, u32[]{:S(2)}, u32[]{:S(2)}) collective-permute-start(bf16[3,296,256]{2,1,0:T(8,128)(2,1)S(1)} %collective-permute-done.8.refs_4_.refs_0_), channel_id=1, source_target_pairs={{0,1},{1,0},{2,3},{3,2},{4,5},{5,4},{6,7},{7,6},{8,9},{9,8},{10,11... | collective-permute-start | bytes 1363976 | tf_op jit(solution)/shard_map/ppermute | solution.py:280
  96.7 17.8 %all-to-all-start.2 = ((f32[32,1,256]{2,1,0:T(1,128)}), f32[32,1,256]{2,1,0:T(1,128)S(1)}, u32[]{:S(2)}, u32[]{:S(2)}) async-start(f32[32,1,256]{2,1,0:T(1,128)} %copy-done.5), calls=%async_computation.2 | async-start | bytes 65536 | tf_op jit(solution)/shard_map/all_to_all | solution.py:18
  117.0 3.3 %copy-start.13 = (bf16[1216,256]{1,0:T(8,128)(2,1)S(1)}, bf16[1216,256]{1,0:T(8,128)(2,1)}, u32[]{:S(2)}) copy-start(bf16[1216,256]{1,0:T(8,128)(2,1)} %copy-done.12) | copy-start | bytes 1867780
  117.0 3.3 %copy-start.15 = (bf16[832,256]{1,0:T(8,128)(2,1)S(1)}, bf16[832,256]{1,0:T(8,128)(2,1)}, u32[]{:S(2)}) copy-start(bf16[832,256]{1,0:T(8,128)(2,1)} %copy-done.14) | copy-start | bytes 1277956
  117.0 3.3 %copy-start.17 = (bf16[832,256]{1,0:T(8,128)(2,1)S(1)}, bf16[832,256]{1,0:T(8,128)(2,1)}, u32[]{:S(2)}) copy-start(bf16[832,256]{1,0:T(8,128)(2,1)} %copy-done.16) | copy-start | bytes 1277956
  117.0 3.3 %copy-start.18 = (s32[16]{0:T(128)S(1)}, s32[16]{0:T(128)}, u32[]{:S(2)}) copy-start(s32[16]{0:T(128)} %slot_ref.3) | copy-start | bytes 196
  120.2 4.5 %collective-permute-start.14 = (f32[256,256]{1,0:T(8,128)S(1)}, f32[256,256]{1,0:T(8,128)S(1)}, u32[]{:S(2)}, u32[]{:S(2)}) collective-permute-start(f32[256,256]{1,0:T(8,128)S(1)} %shard_map.99.hot_ref), channel_id=1, source_target_pairs={{0,1},{1,0},{2,3},{3,2},{4,5},{5,4},{6,7},{7,6},{8,9},{9,8},{10,11... | collective-permute-start | bytes 786440 | tf_op jit(solution)/shard_map/ppermute | solution.py:419
  (13 other events, 17.4 us)

commit v4 on v3

--- a/solution.py
+++ b/solution.py
@@ -243,7 +243,7 @@
 
 def cold_kernel(
     source_ref, slot_ref, me_ref, cold0_ref, cold1_ref, rows0_ref, rows1_ref, err_ref, request_ref,
-    table_ref, hot_ref, new_ref, slots_ref,
+    table_ref, hot_ref, new_hbm, slots_ref, new_ref, sems,
 ):
     rows = table_ref.shape[0]
     peers = request_ref.shape[0]
@@ -264,15 +264,26 @@
         packed_row(request_ref, lambda j: source_ref[n + j], per_peer, 0)
         for n in range(0, peers, group)
     ]
-    chunk_rows = 256
+    chunk_rows, block = 256, rows // sems.shape[0]
     ids = lax.broadcasted_iota(I32, (chunk_rows, LANES), 0)
-    for r in range(0, rows, chunk_rows):
-        place = jnp.concatenate([one_hot(ids + r == row) for row in packed], axis=1)
-        moved = jnp.dot(place, slots_ref[...], preferred_element_type=F32)
-        new_ref[r : r + chunk_rows, :] = table_ref[r : r + chunk_rows, :] - 0.1 * moved
     base = (me_ref[0] // 2) * own_hot
-    for k in range(own_hot):
-        new_ref[pl.ds(slot_ref[k], 1), :] = hot_ref[pl.ds(base + k, 1), :]
+    outs = []
+    for k in range(sems.shape[0]):
+        for r in range(k * block, (k + 1) * block, chunk_rows):
+            place = jnp.concatenate([one_hot(ids + r == row) for row in packed], axis=1)
+            moved = jnp.dot(place, slots_ref[...], preferred_element_type=F32)
+            new_ref[r : r + chunk_rows, :] = table_ref[r : r + chunk_rows, :] - 0.1 * moved
+        for j in range(own_hot):
+            slot = slot_ref[j]
+
+            @pl.when((slot >= k * block) & (slot < (k + 1) * block))
+            def _():
+                new_ref[pl.ds(slot, 1), :] = hot_ref[pl.ds(base + j, 1), :]
+
+        here = slice(k * block, (k + 1) * block)
+        outs += fetch([(new_ref.at[here], new_hbm.at[here])], sems.at[pl.ds(k, 1)])
+    for out in outs:
+        out.wait()
 
 
 def gather_all(x, devices):
@@ -420,13 +431,13 @@
     (new_table,) = call(
         cold_kernel,
         (shape(rows, width, kind=F32),),
-        "sssvvvvvvvvv",
+        "sssvvvvvvvvh",
         [
             source, hot_slot, me[None], cold0, cold1, rows0, rows1, errs, request, table, hot_here,
         ],
         24,
         4 * work,
-        [pltpu.VMEM((slots, width), BF16)],
+        [pltpu.VMEM((slots, width), BF16), pltpu.VMEM((rows, width), F32), copies(4)],
     )
     split = (peers // 2, 1, own_hot, width)
     here, there = hot_here.reshape(split), hot_there.reshape(split)

time: 126 us -> 127 us (level)
  no operation moved by 1% of the time
where the time goes in v4:
time: 127 us; the launch traced here: 126 us
  waiting for transfers between devices  50.8 us (40%)
  Pallas kernels  24.6 us (19%)
  starting transfers between devices  21.7 us (17%)
  blocking collectives  14.3 us (11%)
  local copies, waits for them, and re-layouts  12 us (9%)
  other arithmetic  1.88 us (1%)
    ppermute x14, waiting for transfers between devices, swap(): return lax.ppermute(held, AXES, [(i, i ^ mask(i)) for i in range(devices)])  50.8 us
    pallas_call x7, Pallas kernels, call(): pl.pallas_call(kernel, out_shape=out_shape, in_specs=specs[:len(inputs)],...  24.6 us
    all_to_all x1, blocking collectives, exchange(): return lax.all_to_all(x, AXES, split_axis=0, concat_axis=0, tiled=True)  14.3 us
    ppermute x14, starting transfers between devices, swap(): return lax.ppermute(held, AXES, [(i, i ^ mask(i)) for i in range(devices)])  12.7 us
    unnamed x42, local copies, waits for them, and re-layouts  10.8 us
    all_to_all x2, starting transfers between devices, exchange(): return lax.all_to_all(x, AXES, split_axis=0, concat_axis=0, tiled=True)  8.91 us
  transfers between devices with their start and end apart: 17, of which 9 were waited for; matrix products, arithmetic and copies ran while one was open for 1% of the time, Pallas kernels for 11%

profile of v4, /device:TPU:0, one launch (start us, length us, event | category | flops | bytes accessed | tf_op | source)
XLA Modules:
  0.0 126.2 jit_solution(5963718091546757656)
XLA Ops:
  1.4 14.3 %all_to_all.15.request_ref = s32[32,1,128]{2,1,0:T(1,128)S(1)} all-to-all(s32[32,1,128]{2,1,0:T(1,128)S(1)} %bitcast.56), channel_id=1, replica_groups=mesh['rows'=8,'grp'=4] {'rows','grp'}, dimensions={0} | all-to-all | bytes 32768 | tf_op jit(solution)/shard_map/all_to_all | solution.py:18
  15.7 1.6 %copy-done.8 = f32[2048,256]{1,0:T(8,128)S(1)} copy-done((f32[2048,256]{1,0:T(8,128)S(1)}, f32[2048,256]{1,0:T(8,128)}, u32[]{:S(2)}) %copy-start.8) | copy-done | bytes 2097176
  17.3 3.4 %shard_map.94 = bf16[2048,256]{1,0:T(8,128)(2,1)} custom-call(s32[32,1,128]{2,1,0:T(1,128)S(1)} %all_to_all.15.request_ref, f32[2048,256]{1,0:T(8,128)S(1)} %copy-done.8), custom_call_target="tpu_custom_call" | custom-call | flops 2147483648 | bytes 4194304 | tf_op jit(solution)/shard_map/pallas_call | solution.py:340
  20.8 3.4 %all-to-all-start.1 = ((bf16[32,64,256]{2,1,0:T(8,128)(2,1)}), bf16[32,64,256]{2,1,0:T(8,128)(2,1)}, u32[]{:S(2)}, u32[]{:S(2)}) async-start(bf16[32,64,256]{2,1,0:T(8,128)(2,1)} %bitcast.35), calls=%async_computation.1 | async-start | bytes 2097152 | tf_op jit(solution)/shard_map/all_to_all | solution.py:18
  24.1 2.5 %shard_map.95 = bf16[296,256]{1,0:T(8,128)(2,1)} custom-call(s32[16]{0:T(128)} %slot_ref.3, f32[2048,256]{1,0:T(8,128)} %table_ref.3, f32[256,256]{1,0:T(8,128)} %dense_hbm.3, s32[8,256]{1,0:T(8,128)} %bitcast.43), custom_call_target="tpu_custom_call" | custom-call | flops 1073741824 | bytes 4194304 | tf_op jit(solution)/shard_map/pallas_call | solution.py:340
  26.7 2.6 %collective-permute-start.3 = (bf16[1,296,256]{2,1,0:T(8,128)(2,1)}, bf16[1,296,256]{2,1,0:T(8,128)(2,1)S(1)}, u32[]{:S(2)}, u32[]{:S(2)}) collective-permute-start(bf16[1,296,256]{2,1,0:T(8,128)(2,1)} %bitcast.49), channel_id=1, source_target_pairs={{0,16},{1,17},{2,18},{3,19},{4,20},{5,21},{6,22},{7,23},{8,24},{9,... | collective-permute-start | bytes 454664 | tf_op jit(solution)/shard_map/ppermute | solution.py:291
  29.3 1.5 %collective-permute-start.4 = (bf16[1,296,256]{2,1,0:T(8,128)(2,1)}, bf16[1,296,256]{2,1,0:T(8,128)(2,1)S(1)}, u32[]{:S(2)}, u32[]{:S(2)}) collective-permute-start(bf16[1,296,256]{2,1,0:T(8,128)(2,1)} %bitcast.50), channel_id=1, source_target_pairs={{0,8},{1,9},{2,10},{3,11},{4,12},{5,13},{6,14},{7,15},{8,0},{9,1},... | collective-permute-start | bytes 454664 | tf_op jit(solution)/shard_map/ppermute | solution.py:291
  31.1 29.4 %collective-permute-done.3 = bf16[1,296,256]{2,1,0:T(8,128)(2,1)S(1)} collective-permute-done((bf16[1,296,256]{2,1,0:T(8,128)(2,1)}, bf16[1,296,256]{2,1,0:T(8,128)(2,1)S(1)}, u32[]{:S(2)}, u32[]{:S(2)}) %collective-permute-start.3) | collective-permute-done | bytes 151584 | tf_op jit(solution)/shard_map/ppermute | solution.py:291
  60.6 1.6 %collective-permute-start.6 = (bf16[3,296,256]{2,1,0:T(8,128)(2,1)S(1)}, bf16[3,296,256]{2,1,0:T(8,128)(2,1)S(1)}, u32[]{:S(2)}, u32[]{:S(2)}) collective-permute-start(bf16[3,296,256]{2,1,0:T(8,128)(2,1)S(1)} %constant_dynamic-update-slice_fusion.refs_1_), channel_id=1, source_target_pairs={{0,4},{1,3},{2,6},{3,1},{4,0},{5,7},{6,2},{7,5},{8,12},{9,11},{10,... | collective-permute-start | bytes 1363976 | tf_op jit(solution)/shard_map/ppermute | solution.py:291
  62.7 1.5 %collective-permute-start.7 = (bf16[3,296,256]{2,1,0:T(8,128)(2,1)S(1)}, bf16[3,296,256]{2,1,0:T(8,128)(2,1)S(1)}, u32[]{:S(2)}, u32[]{:S(2)}) collective-permute-start(bf16[3,296,256]{2,1,0:T(8,128)(2,1)S(1)} %constant_dynamic-update-slice_fusion.refs_1_), channel_id=1, source_target_pairs={{0,2},{1,5},{2,0},{3,7},{4,6},{5,1},{6,4},{7,3},{8,10},{9,13},{10,... | collective-permute-start | bytes 1363976 | tf_op jit(solution)/shard_map/ppermute | solution.py:291
  64.2 9.8 %collective-permute-done.6.refs_2_ = bf16[3,296,256]{2,1,0:T(8,128)(2,1)S(1)} collective-permute-done((bf16[3,296,256]{2,1,0:T(8,128)(2,1)S(1)}, bf16[3,296,256]{2,1,0:T(8,128)(2,1)S(1)}, u32[]{:S(2)}, u32[]{:S(2)}) %collective-permute-start.6) | collective-permute-done | bytes 454688 | tf_op jit(solution)/shard_map/ppermute | solution.py:291
  74.0 1.5 %collective-permute-start.8 = (bf16[3,296,256]{2,1,0:T(8,128)(2,1)S(1)}, bf16[3,296,256]{2,1,0:T(8,128)(2,1)S(1)}, u32[]{:S(2)}, u32[]{:S(2)}) collective-permute-start(bf16[3,296,256]{2,1,0:T(8,128)(2,1)S(1)} %collective-permute-done.6.refs_2_), channel_id=1, source_target_pairs={{0,2},{1,5},{2,0},{3,7},{4,6},{5,1},{6,4},{7,3},{8,10},{9,13},{10,... | collective-permute-start | bytes 1363976 | tf_op jit(solution)/shard_map/ppermute | solution.py:291
  76.0 1.2 collective-permute-done
  77.2 1.5 %collective-permute-start.2 = (bf16[1,296,256]{2,1,0:T(8,128)(2,1)S(1)}, bf16[1,296,256]{2,1,0:T(8,128)(2,1)S(1)}, u32[]{:S(2)}, u32[]{:S(2)}) collective-permute-start(bf16[1,296,256]{2,1,0:T(8,128)(2,1)S(1)} %collective-permute-done), channel_id=1, source_target_pairs={{0,2},{1,5},{2,0},{3,7},{4,6},{5,1},{6,4},{7,3},{8,10},{9,13},{10,... | collective-permute-start | bytes 454664 | tf_op jit(solution)/shard_map/ppermute | solution.py:291
  78.7 5.3 %collective-permute-done.1 = bf16[1,296,256]{2,1,0:T(8,128)(2,1)S(1)} collective-permute-done((bf16[1,296,256]{2,1,0:T(8,128)(2,1)}, bf16[1,296,256]{2,1,0:T(8,128)(2,1)S(1)}, u32[]{:S(2)}, u32[]{:S(2)}) %collective-permute-start.1) | collective-permute-done | bytes 151584 | tf_op jit(solution)/shard_map/ppermute | solution.py:291
  84.0 1.6 %collective-permute-done.2 = bf16[1,296,256]{2,1,0:T(8,128)(2,1)S(1)} collective-permute-done((bf16[1,296,256]{2,1,0:T(8,128)(2,1)S(1)}, bf16[1,296,256]{2,1,0:T(8,128)(2,1)S(1)}, u32[]{:S(2)}, u32[]{:S(2)}) %collective-permute-start.2) | collective-permute-done | bytes 151584 | tf_op jit(solution)/shard_map/ppermute | solution.py:291
  88.0 1.4 %collective-permute-done.10.refs_6_.refs_2_ = bf16[3,296,256]{2,1,0:T(8,128)(2,1)S(1)} collective-permute-done((bf16[3,296,256]{2,1,0:T(8,128)(2,1)S(1)}, bf16[3,296,256]{2,1,0:T(8,128)(2,1)S(1)}, u32[]{:S(2)}, u32[]{:S(2)}) %collective-permute-start.10) | collective-permute-done | bytes 454688 | tf_op jit(solution)/shard_map/ppermute | solution.py:291
  92.4 3.7 %shard_map.96 = (f32[256,256]{1,0:T(8,128)}, f32[32,1,256]{2,1,0:T(1,128)S(1)}) custom-call(s32[32]{0:T(128)S(1)} %stack.136.source_ref, bf16[2048,256]{1,0:T(8,128)(2,1)} %bitcast.36.rows_ref, s32[16,128]{1,0:T(8,128)S(1)} %reshape.69.bag_hbm, s32[8,256]{1,0:T(8,128)S(1)} %bitcast.44, f32[256,256]{1,0:T(8,128)S(1)} %copy-done.4, s32[1,256]{1,0:T(1,128)S(1)} %bitcast.45, ...), custom_call_target="tpu_custom_call" | custom-call | flops 1073741824 | bytes 4194304 | tf_op jit(solution)/shard_map/pallas_call | solution.py:340
  96.7 5.5 %all-to-all-start.2 = ((f32[32,1,256]{2,1,0:T(1,128)}), f32[32,1,256]{2,1,0:T(1,128)S(1)}, u32[]{:S(2)}, u32[]{:S(2)}) async-start(f32[32,1,256]{2,1,0:T(1,128)} %copy-done.5), calls=%async_computation.2 | async-start | bytes 65536 | tf_op jit(solution)/shard_map/all_to_all | solution.py:18
  102.5 3.0 %shard_map.97 = (f8e4m3fn[256,3328]{1,0:T(32,128)(4,1)S(1)}, bf16[832,256]{1,0:T(8,128)(2,1)S(1)}, bf16[832,256]{1,0:T(8,128)(2,1)S(1)}) custom-call(s32[13]{0:T(128)S(1)} %stack.137.source_ref, s32[1]{0:T(128)} %bitcast.me_ref, s32[32,1,128]{2,1,0:T(1,128)S(1)} %all_to_all.15.request_ref, bf16[4,296,256]{2,1,0:T(8,128)(2,1)S(1)} %pad_maximum_fusion.refs_0_, ...), custom_call_target="tpu_custom_call" | custom-call | flops 13631488 | bytes 4194304 | tf_op jit(solution)/shard_map/pallas_call | solution.py:340
  107.9 4.0 %shard_map.98 = (f8e4m3fn[256,4864]{1,0:T(32,128)(4,1)S(1)}, bf16[1216,256]{1,0:T(8,128)(2,1)S(1)}, bf16[1216,256]{1,0:T(8,128)(2,1)S(1)}) custom-call(s32[19]{0:T(128)S(1)} %stack.138.source_ref, s32[1]{0:T(128)} %bitcast.me_ref, s32[32,1,128]{2,1,0:T(1,128)S(1)} %all_to_all.15.request_ref, bf16[3,296,256]{2,1,0:T(8,128)(2,1)S(1)} %collective-permute-done.8.refs_4_.refs_0_, ...), custom_call_target="tpu_custom_call" | custom-call | flops 19922944 | bytes 4194304 | tf_op jit(solution)/shard_map/pallas_call | solution.py:340
  114.6 1.3 %copy-done.1 = f8e4m3fn[256,4864]{1,0:T(32,128)(4,1)S(1)} copy-done((f8e4m3fn[256,4864]{1,0:T(32,128)(4,1)S(1)}, f8e4m3fn[256,4864]{1,0:T(32,128)(4,1)}, u32[]{:S(2)}) %copy-start.1) | copy-done | bytes 1245208
  117.0 3.1 %shard_map.99.hot_ref = f32[256,256]{1,0:T(8,128)S(1)} custom-call(s32[32]{0:T(128)S(1)} %stack.136.source_ref, s32[1]{0:T(128)} %bitcast.me_ref, f8e4m3fn[256,3328]{1,0:T(32,128)(4,1)S(1)} %copy-done.3, f8e4m3fn[256,4864]{1,0:T(32,128)(4,1)S(1)} %copy-done.1, f32[32,1,256]{2,1,0:T(1,128)S(1)} %all-to-all-done.2.err_ref, ...), custom_call_target="tpu_custom_call" | custom-call | flops 1073741824 | bytes 4194304 | tf_op jit(solution)/shard_map/pallas_call | solution.py:340
  120.4 4.9 %shard_map.100 = f32[2048,256]{1,0:T(8,128)} custom-call(s32[32]{0:T(128)S(1)} %stack.136.source_ref, s32[16]{0:T(128)S(1)} %copy-done.18, s32[1]{0:T(128)} %bitcast.me_ref, bf16[832,256]{1,0:T(8,128)(2,1)S(1)} %copy-done.15, bf16[1216,256]{1,0:T(8,128)(2,1)S(1)} %copy-done.11, bf16[832,256]{1,0:T(8,128)(2,1)S(1)} %copy-done.17, ...), custom_call_target="tpu_custom_call" | custom-call | flops 4294967296 | bytes 4194304 | tf_op jit(solution)/shard_map/pallas_call | solution.py:340
  (70 shorter events, 15.7 us)
Async XLA Ops:
  20.8 70.7 %all-to-all-start.1 = ((bf16[32,64,256]{2,1,0:T(8,128)(2,1)}), bf16[32,64,256]{2,1,0:T(8,128)(2,1)}, u32[]{:S(2)}, u32[]{:S(2)}) async-start(bf16[32,64,256]{2,1,0:T(8,128)(2,1)} %bitcast.35), calls=%async_computation.1 | async-start | bytes 2097152 | tf_op jit(solution)/shard_map/all_to_all | solution.py:18
  26.6 61.2 %copy-start.19 = (s32[1,32,64]{2,1,0:T(8,128)S(1)}, s32[1,32,64]{2,1,0:T(8,128)}, u32[]{:S(2)}) copy-start(s32[1,32,64]{2,1,0:T(8,128)} %param.10) | copy-start | bytes 24580
  26.7 64.8 %copy-start.6 = (s32[256,8]{0,1:T(8,128)S(1)}, s32[256,8]{0,1:T(8,128)}, u32[]{:S(2)}) copy-start(s32[256,8]{0,1:T(8,128)} %param.11) | copy-start | bytes 24580
  26.7 64.8 %copy-start.7 = (s32[256]{0:T(256)S(1)}, s32[256]{0:T(256)}, u32[]{:S(2)}) copy-start(s32[256]{0:T(256)} %param.13) | copy-start | bytes 3076
  26.7 33.8 %collective-permute-start.3 = (bf16[1,296,256]{2,1,0:T(8,128)(2,1)}, bf16[1,296,256]{2,1,0:T(8,128)(2,1)S(1)}, u32[]{:S(2)}, u32[]{:S(2)}) collective-permute-start(bf16[1,296,256]{2,1,0:T(8,128)(2,1)} %bitcast.49), channel_id=1, source_target_pairs={{0,16},{1,17},{2,18},{3,19},{4,20},{5,21},{6,22},{7,23},{8,24},{9,... | collective-permute-start | bytes 454664 | tf_op jit(solution)/shard_map/ppermute | solution.py:291
  29.3 31.2 %collective-permute-start.4 = (bf16[1,296,256]{2,1,0:T(8,128)(2,1)}, bf16[1,296,256]{2,1,0:T(8,128)(2,1)S(1)}, u32[]{:S(2)}, u32[]{:S(2)}) collective-permute-start(bf16[1,296,256]{2,1,0:T(8,128)(2,1)} %bitcast.50), channel_id=1, source_target_pairs={{0,8},{1,9},{2,10},{3,11},{4,12},{5,13},{6,14},{7,15},{8,0},{9,1},... | collective-permute-start | bytes 454664 | tf_op jit(solution)/shard_map/ppermute | solution.py:291
  30.9 29.7 %collective-permute-start.5 = (bf16[1,296,256]{2,1,0:T(8,128)(2,1)}, bf16[1,296,256]{2,1,0:T(8,128)(2,1)S(1)}, u32[]{:S(2)}, u32[]{:S(2)}) collective-permute-start(bf16[1,296,256]{2,1,0:T(8,128)(2,1)} %bitcast.51), channel_id=1, source_target_pairs={{0,24},{1,25},{2,26},{3,27},{4,28},{5,29},{6,30},{7,31},{8,16},{9,... | collective-permute-start | bytes 454664 | tf_op jit(solution)/shard_map/ppermute | solution.py:291
  60.6 13.4 %collective-permute-start.6 = (bf16[3,296,256]{2,1,0:T(8,128)(2,1)S(1)}, bf16[3,296,256]{2,1,0:T(8,128)(2,1)S(1)}, u32[]{:S(2)}, u32[]{:S(2)}) collective-permute-start(bf16[3,296,256]{2,1,0:T(8,128)(2,1)S(1)} %constant_dynamic-update-slice_fusion.refs_1_), channel_id=1, source_target_pairs={{0,4},{1,3},{2,6},{3,1},{4,0},{5,7},{6,2},{7,5},{8,12},{9,11},{10,... | collective-permute-start | bytes 1363976 | tf_op jit(solution)/shard_map/ppermute | solution.py:291
  62.2 15.1 %collective-permute-start = (bf16[1,296,256]{2,1,0:T(8,128)(2,1)}, bf16[1,296,256]{2,1,0:T(8,128)(2,1)S(1)}, u32[]{:S(2)}, u32[]{:S(2)}) collective-permute-start(bf16[1,296,256]{2,1,0:T(8,128)(2,1)} %bitcast.52), channel_id=1, source_target_pairs={{0,4},{1,3},{2,6},{3,1},{4,0},{5,7},{6,2},{7,5},{8,12},{9,11},{10,... | collective-permute-start | bytes 454664 | tf_op jit(solution)/shard_map/ppermute | solution.py:291
  62.7 24.6 %collective-permute-start.7 = (bf16[3,296,256]{2,1,0:T(8,128)(2,1)S(1)}, bf16[3,296,256]{2,1,0:T(8,128)(2,1)S(1)}, u32[]{:S(2)}, u32[]{:S(2)}) collective-permute-start(bf16[3,296,256]{2,1,0:T(8,128)(2,1)S(1)} %constant_dynamic-update-slice_fusion.refs_1_), channel_id=1, source_target_pairs={{0,2},{1,5},{2,0},{3,7},{4,6},{5,1},{6,4},{7,3},{8,10},{9,13},{10,... | collective-permute-start | bytes 1363976 | tf_op jit(solution)/shard_map/ppermute | solution.py:291
  74.0 13.8 %collective-permute-start.8 = (bf16[3,296,256]{2,1,0:T(8,128)(2,1)S(1)}, bf16[3,296,256]{2,1,0:T(8,128)(2,1)S(1)}, u32[]{:S(2)}, u32[]{:S(2)}) collective-permute-start(bf16[3,296,256]{2,1,0:T(8,128)(2,1)S(1)} %collective-permute-done.6.refs_2_), channel_id=1, source_target_pairs={{0,2},{1,5},{2,0},{3,7},{4,6},{5,1},{6,4},{7,3},{8,10},{9,13},{10,... | collective-permute-start | bytes 1363976 | tf_op jit(solution)/shard_map/ppermute | solution.py:291
  75.4 8.6 %collective-permute-start.1 = (bf16[1,296,256]{2,1,0:T(8,128)(2,1)}, bf16[1,296,256]{2,1,0:T(8,128)(2,1)S(1)}, u32[]{:S(2)}, u32[]{:S(2)}) collective-permute-start(bf16[1,296,256]{2,1,0:T(8,128)(2,1)} %bitcast.53), channel_id=1, source_target_pairs={{0,2},{1,5},{2,0},{3,7},{4,6},{5,1},{6,4},{7,3},{8,10},{9,13},{10,... | collective-permute-start | bytes 454664 | tf_op jit(solution)/shard_map/ppermute | solution.py:291
  77.2 8.4 %collective-permute-start.2 = (bf16[1,296,256]{2,1,0:T(8,128)(2,1)S(1)}, bf16[1,296,256]{2,1,0:T(8,128)(2,1)S(1)}, u32[]{:S(2)}, u32[]{:S(2)}) collective-permute-start(bf16[1,296,256]{2,1,0:T(8,128)(2,1)S(1)} %collective-permute-done), channel_id=1, source_target_pairs={{0,2},{1,5},{2,0},{3,7},{4,6},{5,1},{6,4},{7,3},{8,10},{9,13},{10,... | collective-permute-start | bytes 454664 | tf_op jit(solution)/shard_map/ppermute | solution.py:291
  86.6 2.7 %collective-permute-start.9 = (bf16[4,296,256]{2,1,0:T(8,128)(2,1)S(1)}, bf16[4,296,256]{2,1,0:T(8,128)(2,1)S(1)}, u32[]{:S(2)}, u32[]{:S(2)}) collective-permute-start(bf16[4,296,256]{2,1,0:T(8,128)(2,1)S(1)} %pad_maximum_fusion.refs_0_), channel_id=1, source_target_pairs={{0,1},{1,0},{2,3},{3,2},{4,5},{5,4},{6,7},{7,6},{8,9},{9,8},{10,11... | collective-permute-start | bytes 1818632 | tf_op jit(solution)/shard_map/ppermute | solution.py:291
  86.7 2.7 %collective-permute-start.10 = (bf16[3,296,256]{2,1,0:T(8,128)(2,1)S(1)}, bf16[3,296,256]{2,1,0:T(8,128)(2,1)S(1)}, u32[]{:S(2)}, u32[]{:S(2)}) collective-permute-start(bf16[3,296,256]{2,1,0:T(8,128)(2,1)S(1)} %constant_dynamic-update-slice_fusion.refs_1_), channel_id=1, source_target_pairs={{0,1},{1,0},{2,3},{3,2},{4,5},{5,4},{6,7},{7,6},{8,9},{9,8},{10,11... | collective-permute-start | bytes 1363976 | tf_op jit(solution)/shard_map/ppermute | solution.py:291
  87.2 2.9 %collective-permute-start.11 = (bf16[3,296,256]{2,1,0:T(8,128)(2,1)S(1)}, bf16[3,296,256]{2,1,0:T(8,128)(2,1)}, u32[]{:S(2)}, u32[]{:S(2)}) collective-permute-start(bf16[3,296,256]{2,1,0:T(8,128)(2,1)S(1)} %collective-permute-done.6.refs_2_), channel_id=1, source_target_pairs={{0,1},{1,0},{2,3},{3,2},{4,5},{5,4},{6,7},{7,6},{8,9},{9,8},{10,11... | collective-permute-start | bytes 1363976 | tf_op jit(solution)/shard_map/ppermute | solution.py:291
  87.3 3.5 %collective-permute-start.12 = (bf16[3,296,256]{2,1,0:T(8,128)(2,1)S(1)}, bf16[3,296,256]{2,1,0:T(8,128)(2,1)}, u32[]{:S(2)}, u32[]{:S(2)}) collective-permute-start(bf16[3,296,256]{2,1,0:T(8,128)(2,1)S(1)} %collective-permute-done.7.refs_3_), channel_id=1, source_target_pairs={{0,1},{1,0},{2,3},{3,2},{4,5},{5,4},{6,7},{7,6},{8,9},{9,8},{10,11... | collective-permute-start | bytes 1363976 | tf_op jit(solution)/shard_map/ppermute | solution.py:291
  87.7 3.7 %collective-permute-start.13 = (bf16[3,296,256]{2,1,0:T(8,128)(2,1)S(1)}, bf16[3,296,256]{2,1,0:T(8,128)(2,1)}, u32[]{:S(2)}, u32[]{:S(2)}) collective-permute-start(bf16[3,296,256]{2,1,0:T(8,128)(2,1)S(1)} %collective-permute-done.8.refs_4_.refs_0_), channel_id=1, source_target_pairs={{0,1},{1,0},{2,3},{3,2},{4,5},{5,4},{6,7},{7,6},{8,9},{9,8},{10,11... | collective-permute-start | bytes 1363976 | tf_op jit(solution)/shard_map/ppermute | solution.py:291
  96.7 17.8 %all-to-all-start.2 = ((f32[32,1,256]{2,1,0:T(1,128)}), f32[32,1,256]{2,1,0:T(1,128)S(1)}, u32[]{:S(2)}, u32[]{:S(2)}) async-start(f32[32,1,256]{2,1,0:T(1,128)} %copy-done.5), calls=%async_computation.2 | async-start | bytes 65536 | tf_op jit(solution)/shard_map/all_to_all | solution.py:18
  117.0 3.3 %copy-start.13 = (bf16[1216,256]{1,0:T(8,128)(2,1)S(1)}, bf16[1216,256]{1,0:T(8,128)(2,1)}, u32[]{:S(2)}) copy-start(bf16[1216,256]{1,0:T(8,128)(2,1)} %copy-done.12) | copy-start | bytes 1867780
  117.0 3.3 %copy-start.15 = (bf16[832,256]{1,0:T(8,128)(2,1)S(1)}, bf16[832,256]{1,0:T(8,128)(2,1)}, u32[]{:S(2)}) copy-start(bf16[832,256]{1,0:T(8,128)(2,1)} %copy-done.14) | copy-start | bytes 1277956
  117.0 3.3 %copy-start.17 = (bf16[832,256]{1,0:T(8,128)(2,1)S(1)}, bf16[832,256]{1,0:T(8,128)(2,1)}, u32[]{:S(2)}) copy-start(bf16[832,256]{1,0:T(8,128)(2,1)} %copy-done.16) | copy-start | bytes 1277956
  117.0 3.3 %copy-start.18 = (s32[16]{0:T(128)S(1)}, s32[16]{0:T(128)}, u32[]{:S(2)}) copy-start(s32[16]{0:T(128)} %slot_ref.3) | copy-start | bytes 196
  120.2 5.1 %collective-permute-start.14 = (f32[256,256]{1,0:T(8,128)S(1)}, f32[256,256]{1,0:T(8,128)S(1)}, u32[]{:S(2)}, u32[]{:S(2)}) collective-permute-start(f32[256,256]{1,0:T(8,128)S(1)} %shard_map.99.hot_ref), channel_id=1, source_target_pairs={{0,1},{1,0},{2,3},{3,2},{4,5},{5,4},{6,7},{7,6},{8,9},{9,8},{10,11... | collective-permute-start | bytes 786440 | tf_op jit(solution)/shard_map/ppermute | solution.py:430
  (13 other events, 17.4 us)
